TPU v7x, 512 devices: a whole 4x4x16 slice. The times are simulated.
512 devices in a mesh: gx: 16 (over y, x), gy: 32 (over z, core).
Axes of the slice: x: 4, y: 4, z: 16, core: 2. Of those that a mesh axis runs over, the one named last changes fastest.
Arguments:
- surface: float32 [1024, 16384], P('gx', 'gy'), may hold values from -6 to 6
- east_velocity: float32 [1024, 16384], P('gx', 'gy'), may hold values from -3 to 3
- north_velocity: float32 [1024, 16384], P('gx', 'gy'), may hold values from -3 to 3
- east_depth: float32 [1024, 16384], P('gx', 'gy'), may hold values from 0.25 to 2
- north_depth: float32 [1024, 16384], P('gx', 'gy'), may hold values from 0.25 to 2
- slot_gauge: int32 [512, 128], P(('gx', 'gy')), may hold values from 0 to 32768, as said below
- slot_cell: int32 [512, 128], P(('gx', 'gy')), may hold values from 0 to 32767
Outputs:
- final_surface: float32 [1024, 16384], P('gx', 'gy')
- final_east: float32 [1024, 16384], P('gx', 'gy')
- final_north: float32 [1024, 16384], P('gx', 'gy')
- gauge_series: float32 [32768, 48], P(('gx', 'gy'))
Inputs may be any that keep to these rules, and one draw needn't show every extreme that they name: `slot_gauge`: entries below 32768 are gauge ids: every id 0 to 32767 stands exactly once in the whole array, in the row of the device whose block holds that gauge; the ids owned by device d, d * 64 to (d + 1) * 64 - 1, all lie in blocks with d's gx index. Each row lists its ids first, then 32768 in the unused slots. Some device's row is full in every draw.
All inputs are finite; a program needn't handle non-finite values.
Results may differ from a plain program's by a relative error of at most 0.00012.
Values sent between devices are 32-bit elements; how exact they have to be, the bound alone decides.
No kernel may reach another device: no remote copies, remote signals or barrier semaphores. Data moves between devices by JAX's collectives and lax.ppermute only.
A program may use at most 64 MiB of HBM per device.

v0:
```python
import jax
import jax.numpy as jnp
from jax import lax
from jax.sharding import PartitionSpec as P

STEPS = 16
GAUGE_DEV = 64


time_step = 0.45


def with_halo(cells, sides, width):
    for axis, dim in sides:
        count = lax.axis_size(axis)
        ends = count - 1
        head = lax.slice_in_dim(cells, 0, width, axis=dim)
        tail = lax.slice_in_dim(cells, cells.shape[dim] - width, cells.shape[dim], axis=dim)
        cells = jnp.concatenate(
            [
                lax.ppermute(tail, axis, [(i, (i + 1) % count) for i in range(ends)]),
                cells,
                lax.ppermute(head, axis, [((i + 1) % count, i) for i in range(ends)]),
            ],
            axis=dim,
        )
    return cells


def in_blocks(array, dim, size):
    before, after = (array.shape[:dim], array.shape[dim + 1 :])
    return jnp.moveaxis(array.reshape(*before, size, -1, *after), dim, 0)


def sent_and_summed(array, axis, dim):
    blocks = in_blocks(array, dim, lax.axis_size(axis))
    arrived = lax.all_to_all(blocks, axis, split_axis=0, concat_axis=0, tiled=True)
    return arrived.sum(axis=0)


def update_velocity(eta, east, north, below, right):
    eta_down = jnp.concatenate([eta[1:], below], 0)
    eta_right = jnp.concatenate([eta[:, 1:], right], 1)
    east = east - time_step * (eta_down - eta)
    north = north - time_step * (eta_right - eta)
    return (east, north)


def update_surface(eta, flux_x, flux_y, above, left):
    flux_up = jnp.concatenate([above, flux_x[:-1]], 0)
    flux_left = jnp.concatenate([left, flux_y[:, :-1]], 1)
    return eta - time_step * (flux_x - flux_up + flux_y - flux_left)


def advance_margin(eta, east, north, east_depth, north_depth, inside):
    east, north = update_velocity(
        eta, east, north, jnp.zeros_like(eta[:1]), jnp.zeros_like(eta[:, :1])
    )
    east = east * inside
    north = north * inside
    flux_x = east_depth * east
    flux_y = north_depth * north
    eta = update_surface(
        eta, flux_x, flux_y, jnp.zeros_like(flux_x[:1]), jnp.zeros_like(flux_y[:, :1])
    )
    return (eta * inside, east, north)


def sample_cells(fields, row_pick, col_pick):
    picked = []
    for field in fields:
        rows_taken = jnp.dot(row_pick, field, precision=lax.Precision.HIGHEST)
        picked.append(jnp.sum(rows_taken * col_pick, axis=1))
    return jnp.stack(picked)


def shards(surface, east_velocity, north_velocity, east_depth, north_depth, slot_gauge, slot_cell):
    rows_dev, cols_dev = surface.shape
    slot_ids = slot_gauge.reshape(-1)
    cells = slot_cell.reshape(-1)
    count = slot_ids.shape[0]

    def record_step(records, step, fields, row_pick, col_pick):
        taken = sample_cells(fields, row_pick, col_pick)
        return lax.dynamic_update_slice_in_dim(records, taken[:, None, :], step, 1)

    records = jnp.zeros((3, STEPS, count), jnp.float32)
    margin = STEPS
    stacked = jnp.stack([surface, east_velocity, north_velocity, east_depth, north_depth])
    widened = with_halo(stacked, (("gx", 1), ("gy", 2)), STEPS)
    row_ids = (
        lax.axis_index("gx") * rows_dev
        - margin
        + jnp.arange(rows_dev + 2 * margin, dtype=jnp.int32)
    )
    col_ids = (
        lax.axis_index("gy") * cols_dev
        - margin
        + jnp.arange(cols_dev + 2 * margin, dtype=jnp.int32)
    )
    row_inside = (row_ids >= 0) & (row_ids < rows_dev * lax.axis_size("gx"))
    col_inside = (col_ids >= 0) & (col_ids < cols_dev * lax.axis_size("gy"))
    inside = (row_inside[:, None] & col_inside[None, :]).astype(jnp.float32)
    depth_x = widened[3]
    depth_y = widened[4]
    pickers_row_pick = (
        (cells // cols_dev + margin)[:, None]
        == jnp.arange(rows_dev + 2 * margin, dtype=jnp.int32)[None, :]
    ).astype(jnp.float32)
    pickers_col_pick = (
        (cells % cols_dev + margin)[:, None]
        == jnp.arange(cols_dev + 2 * margin, dtype=jnp.int32)[None, :]
    ).astype(jnp.float32)
    row_pick = pickers_row_pick
    col_pick = pickers_col_pick

    def turn(step, carry):
        eta, east, north, kept = carry
        eta, east, north = advance_margin(eta, east, north, depth_x, depth_y, inside)
        kept = record_step(kept, step, (eta, east, north), row_pick, col_pick)
        return (eta, east, north, kept)

    eta, east, north, records = lax.fori_loop(
        0, STEPS, turn, (widened[0], widened[1], widened[2], records)
    )
    eta = eta[margin : margin + rows_dev, margin : margin + cols_dev]
    east = east[margin : margin + rows_dev, margin : margin + cols_dev]
    north = north[margin : margin + rows_dev, margin : margin + cols_dev]
    flat_records = records.reshape(3 * STEPS, count)
    band = lax.axis_size("gy") * GAUGE_DEV
    local_ids = slot_ids - lax.axis_index("gx") * band
    placer = (local_ids[:, None] == jnp.arange(band, dtype=jnp.int32)[None, :]).astype(jnp.float32)
    placed = lax.dot_general(
        placer, flat_records, (((0,), (1,)), ((), ())), precision=lax.Precision.HIGHEST
    )
    series = sent_and_summed(placed, "gy", 0)
    return (eta, east, north, series)


def solution(mesh):
    in_specs = (
        P("gx", "gy"),
        P("gx", "gy"),
        P("gx", "gy"),
        P("gx", "gy"),
        P("gx", "gy"),
        P(("gx", "gy"), None),
        P(("gx", "gy"), None),
    )
    out_specs = (P("gx", "gy"), P("gx", "gy"), P("gx", "gy"), P(("gx", "gy"), None))
    return jax.shard_map(shards, mesh=mesh, in_specs=in_specs, out_specs=out_specs, check_vma=False)
```

profile of v0, /device:TPU:24, one launch (start us, length us, event | category | flops | bytes accessed | tf_op | source)
XLA Modules:
  0.0 121.9 jit_solution(12199873008018926150)
XLA Ops:
  0.7 0.9 bitcast_dynamic-update-slice_fusion.4
  1.6 0.9 bitcast_dynamic-update-slice_fusion.3
  2.5 0.9 bitcast_dynamic-update-slice_fusion.2
  3.4 0.9 bitcast_dynamic-update-slice_fusion.1
  4.3 0.9 bitcast_dynamic-update-slice_fusion
  5.3 3.4 %collective-permute-start = (f32[5,16,512]{2,1,0:T(8,128)S(1)}, f32[5,16,512]{2,1,0:T(8,128)S(1)}, u32[]{:S(2)}, u32[]{:S(2)}) collective-permute-start(f32[5,16,512]{2,1,0:T(8,128)S(1)} %get-tuple-element.245), channel_id=1, source_target_pairs={{0,32},{32,64},{64,96},{96,128},{128,160},{160,192},{192,224},{224... | collective-permute-start | bytes 491528 | tf_op jit(solution)/shard_map/ppermute | solution.py:21
  8.7 4.6 %collective-permute-start.1 = (f32[5,16,512]{2,1,0:T(8,128)S(1)}, f32[5,16,512]{2,1,0:T(8,128)S(1)}, u32[]{:S(2)}, u32[]{:S(2)}) collective-permute-start(f32[5,16,512]{2,1,0:T(8,128)S(1)} %get-tuple-element.246), channel_id=1, source_target_pairs={{32,0},{64,32},{96,64},{128,96},{160,128},{192,160},{224,192},{256... | collective-permute-start | bytes 491528 | tf_op jit(solution)/shard_map/ppermute | solution.py:23
  13.4 1.9 %collective-permute-done = f32[5,16,512]{2,1,0:T(8,128)S(1)} collective-permute-done((f32[5,16,512]{2,1,0:T(8,128)S(1)}, f32[5,16,512]{2,1,0:T(8,128)S(1)}, u32[]{:S(2)}, u32[]{:S(2)}) %collective-permute-start) | collective-permute-done | bytes 163872 | tf_op jit(solution)/shard_map/ppermute | solution.py:21
  15.2 1.2 collective-permute-done.1
  16.6 1.3 %collective-permute-start.2 = (f32[5,96,16]{2,1,0:T(8,128)S(1)}, f32[5,96,16]{2,1,0:T(8,128)S(1)}, u32[]{:S(2)}, u32[]{:S(2)}) collective-permute-start(f32[5,96,16]{2,1,0:T(8,128)S(1)} %get-tuple-element.243), channel_id=1, source_target_pairs={{0,1},{1,2},{2,3},{3,4},{4,5},{5,6},{6,7},{7,8},{8,9},{9,10},{10,1... | collective-permute-start | bytes 92168 | tf_op jit(solution)/shard_map/ppermute | solution.py:21
  17.9 1.3 %collective-permute-start.3 = (f32[5,96,16]{2,1,0:T(8,128)S(1)}, f32[5,96,16]{2,1,0:T(8,128)S(1)}, u32[]{:S(2)}, u32[]{:S(2)}) collective-permute-start(f32[5,96,16]{2,1,0:T(8,128)S(1)} %get-tuple-element.244), channel_id=1, source_target_pairs={{1,0},{2,1},{3,2},{4,3},{5,4},{6,5},{7,6},{8,7},{9,8},{10,9},{11,1... | collective-permute-start | bytes 92168 | tf_op jit(solution)/shard_map/ppermute | solution.py:23
  19.2 4.2 %collective-permute-done.3 = f32[5,96,16]{2,1,0:T(8,128)S(1)} collective-permute-done((f32[5,96,16]{2,1,0:T(8,128)S(1)}, f32[5,96,16]{2,1,0:T(8,128)S(1)}, u32[]{:S(2)}, u32[]{:S(2)}) %collective-permute-start.3) | collective-permute-done | bytes 30752 | tf_op jit(solution)/shard_map/ppermute | solution.py:23
  23.9 44.3 %while.20 = (s32[]{:T(128)}, f32[96,544]{1,0:T(8,128)S(1)}, f32[96,544]{1,0:T(8,128)S(1)}, f32[96,544]{1,0:T(8,128)S(1)}, f32[3,16,128]{2,1,0:T(8,128)S(1)}, /*i...) while((s32[]{:T(128)}, f32[96,544]{1,0:T(8,128)S(1)}, ...), condition=%wide.region_4.5_spmd.clone, body=%wide.region_0.4_spmd.clone.sunk | while | flops 242289024 | bytes 5018497 | solution.py:123
  25.2 0.7 fusion.54
  25.9 0.7 fusion.55
  28.0 0.7 fusion.54
  30.7 0.7 fusion.54
  31.5 0.7 fusion.55
  33.5 0.7 fusion.54
  34.2 0.7 fusion.55
  36.3 0.7 fusion.54
  37.0 0.7 fusion.55
  39.8 0.7 fusion.55
  41.8 0.7 fusion.54
  68.3 1.7 %fusion.30 = f32[32,48,64]{2,1,0:T(8,128)S(1)} fusion(f32[48,128,1]{1,0,2:T(8,128)S(1)} %bitcast.101, s32[32,64]{1,0:T(8,128)S(1)} %multiply_add_fusion, s32[128]{0:T(128)S(1)} %subtract_bitcast_fusion), kind=kOutput, calls=%fused_computation.60 | convolution fusion | flops 151257088 | bytes 426496 | tf_op jit(solution)/shard_map/dot_general | solution.py:133
  70.0 1.2 %reshape.108 = f32[32,1,3072]{2,1,0:T(1,128)} reshape(f32[32,48,64]{2,1,0:T(8,128)S(1)} %fusion.30) | data formatting | bytes 786432
  71.2 19.6 %all-to-all-start = ((f32[32,1,3072]{2,1,0:T(1,128)}), f32[32,1,3072]{2,1,0:T(1,128)S(1)}, u32[]{:S(2)}, u32[]{:S(2)}) async-start(f32[32,1,3072]{2,1,0:T(1,128)} %reshape.108), calls=%async_computation | async-start | bytes 786432 | tf_op jit(solution)/shard_map/all_to_all | solution.py:37
  90.7 0.8 slice.73
  91.5 0.8 slice.74
  92.3 0.8 slice.75
  93.0 25.9 %all-to-all-done = f32[32,1,3072]{2,1,0:T(1,128)S(1)} async-done(((f32[32,1,3072]{2,1,0:T(1,128)}), f32[32,1,3072]{2,1,0:T(1,128)S(1)}, u32[]{:S(2)}, u32[]{:S(2)}) %all-to-all-start) | async-done | bytes 393248 | tf_op jit(solution)/shard_map/all_to_all | solution.py:37
  119.5 1.6 %reduce = f32[32,3072]{1,0:T(8,128)S(1)} reduce(f32[32,1,3072]{2,1,0:T(1,128)S(1)} %all-to-all-done, f32[]{:T(128)} %broadcast.174), dimensions={1}, to_apply=%all_to_all.3.reduce_sub_computation | reduce | bytes 786436 | tf_op jit(solution)/shard_map/all_to_all | solution.py:37
  (167 shorter events, 37.6 us)
Async XLA Ops:
  0.6 12.6 %copy-start = (s32[1,128]{1,0:T(1,128)S(1)}, s32[1,128]{1,0:T(1,128)}, u32[]{:S(2)}) copy-start(s32[1,128]{1,0:T(1,128)} %param.15) | copy-start | bytes 1540
  0.6 12.7 %copy-start.1 = (s32[1,128]{1,0:T(1,128)S(1)}, s32[1,128]{1,0:T(1,128)}, u32[]{:S(2)}) copy-start(s32[1,128]{1,0:T(1,128)} %param.14) | copy-start | bytes 1540
  5.3 9.9 %collective-permute-start = (f32[5,16,512]{2,1,0:T(8,128)S(1)}, f32[5,16,512]{2,1,0:T(8,128)S(1)}, u32[]{:S(2)}, u32[]{:S(2)}) collective-permute-start(f32[5,16,512]{2,1,0:T(8,128)S(1)} %get-tuple-element.245), channel_id=1, source_target_pairs={{0,32},{32,64},{64,96},{96,128},{128,160},{160,192},{192,224},{224... | collective-permute-start | bytes 491528 | tf_op jit(solution)/shard_map/ppermute | solution.py:21
  8.7 7.7 %collective-permute-start.1 = (f32[5,16,512]{2,1,0:T(8,128)S(1)}, f32[5,16,512]{2,1,0:T(8,128)S(1)}, u32[]{:S(2)}, u32[]{:S(2)}) collective-permute-start(f32[5,16,512]{2,1,0:T(8,128)S(1)} %get-tuple-element.246), channel_id=1, source_target_pairs={{32,0},{64,32},{96,64},{128,96},{160,128},{192,160},{224,192},{256... | collective-permute-start | bytes 491528 | tf_op jit(solution)/shard_map/ppermute | solution.py:23
  16.6 2.6 %collective-permute-start.2 = (f32[5,96,16]{2,1,0:T(8,128)S(1)}, f32[5,96,16]{2,1,0:T(8,128)S(1)}, u32[]{:S(2)}, u32[]{:S(2)}) collective-permute-start(f32[5,96,16]{2,1,0:T(8,128)S(1)} %get-tuple-element.243), channel_id=1, source_target_pairs={{0,1},{1,2},{2,3},{3,4},{4,5},{5,6},{6,7},{7,8},{8,9},{9,10},{10,1... | collective-permute-start | bytes 92168 | tf_op jit(solution)/shard_map/ppermute | solution.py:21
  17.9 5.5 %collective-permute-start.3 = (f32[5,96,16]{2,1,0:T(8,128)S(1)}, f32[5,96,16]{2,1,0:T(8,128)S(1)}, u32[]{:S(2)}, u32[]{:S(2)}) collective-permute-start(f32[5,96,16]{2,1,0:T(8,128)S(1)} %get-tuple-element.244), channel_id=1, source_target_pairs={{1,0},{2,1},{3,2},{4,3},{5,4},{6,5},{7,6},{8,7},{9,8},{10,9},{11,1... | collective-permute-start | bytes 92168 | tf_op jit(solution)/shard_map/ppermute | solution.py:23
  71.2 47.8 %all-to-all-start = ((f32[32,1,3072]{2,1,0:T(1,128)}), f32[32,1,3072]{2,1,0:T(1,128)S(1)}, u32[]{:S(2)}, u32[]{:S(2)}) async-start(f32[32,1,3072]{2,1,0:T(1,128)} %reshape.108), calls=%async_computation | async-start | bytes 786432 | tf_op jit(solution)/shard_map/all_to_all | solution.py:37
where the time goes:
time: 124 us; the launch traced here: 122 us
  matrix products  36.1 us (29%)
  waiting for transfers between devices  33.2 us (27%)
  starting transfers between devices  30.1 us (24%)
  local copies, waits for them, and re-layouts  12 us (10%)
  other arithmetic  8.81 us (7%)
    dot_general x48, matrix products, sample_cells(): rows_taken = jnp.dot(row_pick, field, precision=lax.Precision.HIGHEST)  34.4 us
    all_to_all x1, waiting for transfers between devices, sent_and_summed(): lax.all_to_all(blocks, axis, split_axis=0, concat_axis=0, tiled=True)  25.9 us
    all_to_all x1, starting transfers between devices, sent_and_summed(): lax.all_to_all(blocks, axis, split_axis=0, concat_axis=0, tiled=True)  19.6 us
    ppermute x2, starting transfers between devices, with_halo(): lax.ppermute(head, axis, [((i + 1) % count, i) for i in range(ends)])  5.84 us
    ppermute x2, waiting for transfers between devices, with_halo(): lax.ppermute(head, axis, [((i + 1) % count, i) for i in range(ends)])  5.39 us
    unnamed x10, local copies, waits for them, and re-layouts  5.11 us
    ppermute x2, starting transfers between devices, with_halo(): lax.ppermute(tail, axis, [(i, (i + 1) % count) for i in range(ends)])  4.7 us
    mul x16, other arithmetic, advance_margin(): return (eta * inside, east, north)  3.23 us
  transfers between devices with their start and end apart: 5, of which 4 were waited for; matrix products, arithmetic and copies ran while one was open for 2% of the time, Pallas kernels for 0%

commit v1 on v0

v1 whole, which is shorter than its diff:
```python
import functools

import jax
import jax.numpy as jnp
from jax import lax
from jax.experimental import pallas as pl
from jax.experimental.pallas import tpu as pltpu
from jax.sharding import PartitionSpec as P

STEPS = 16
GAUGE_DEV = 64
QUAD = 4
LANES = 128
DT = 0.45


def lane_ids(shape):
    return lax.broadcasted_iota(jnp.int32, shape, 1)


def pack_columns_kernel(e, u, v, dx, dy, top, bot, head, tail, *, margin):
    rows, cols = e.shape
    lane = lane_ids((margin, LANES))
    last = cols - LANES
    fields = (e, u, v, dx, dy)
    for r in range(0, rows + 2 * margin, margin):
        out_head = jnp.zeros((margin, LANES), jnp.float32)
        out_tail = jnp.zeros((margin, LANES), jnp.float32)
        for f, ref in enumerate(fields):
            if r == 0:
                src, at = top, f * margin
            elif r == rows + margin:
                src, at = bot, f * margin
            else:
                src, at = ref, r - margin
            first = src[at : at + margin, :LANES]
            final = src[at : at + margin, last:]
            mine = (lane >= margin * f) & (lane < margin * (f + 1))
            if f:
                first = pltpu.roll(first, margin * f, 1)
            final = pltpu.roll(final, (margin * f + margin) % LANES, 1)
            out_head = jnp.where(mine, first, out_head)
            out_tail = jnp.where(mine, final, out_tail)
        head[r : r + margin, :] = out_head
        tail[r : r + margin, :] = out_tail


def steps_kernel(
    cells, edges, ids, e, u, v, dx, dy, top, bot, from_left, from_right,
    out_e, out_u, out_v, out_rec, he, hu, hv, sx, sy, *, steps,
):
    rows, cols = e.shape
    margin = steps
    own = cols // LANES
    tiles = own + 1
    height = rows + 2 * margin
    pitch = height + 8
    chunk = 16
    lane = lane_ids((chunk, LANES))

    for f, (ref, dst, base) in enumerate(
        ((e, he, 0), (u, hu, 0), (v, hv, 0), (dx, sx, 8), (dy, sy, 8))
    ):
        for j in range(own):
            cut = slice(LANES * j, LANES * (j + 1))
            dst[j, base : base + margin, :] = top[f * margin : (f + 1) * margin, cut]
            dst[j, base + margin : base + margin + rows, :] = ref[:, cut]
            dst[j, base + margin + rows : base + height, :] = bot[f * margin : (f + 1) * margin, cut]
        for r in range(0, height, chunk):
            right = from_right[r : r + chunk, :]
            left = from_left[r : r + chunk, :]
            if f:
                right = pltpu.roll(right, LANES - margin * f, 1)
            left = pltpu.roll(left, (LANES - margin - margin * f) % LANES, 1)
            tile = jnp.where(
                lane < margin, right, jnp.where(lane >= LANES - margin, left, jnp.zeros_like(left))
            )
            dst[own, base + r : base + r + chunk, :] = tile

    keep_rows = edges[0] == 0
    keep_cols = (lane >= LANES // 2) | (edges[1] == 0)

    for s in range(steps):
        low = (s // 8) * 8
        high = height - low
        now, new = s * pitch, (s + 1) * pitch
        for r in range(low, high, chunk):
            size = min(chunk, high - r)
            at_edge = lane[:size] == LANES - 1
            eta = [he[j, now + r : now + r + size, :] for j in range(tiles)]
            turned = [pltpu.roll(t, LANES - 1, 1) for t in eta]
            for j in range(tiles):
                down = he[j, now + r + 1 : now + r + 1 + size, :]
                right = jnp.where(at_edge, turned[(j + 1) % tiles], turned[j])
                hu[j, new + r : new + r + size, :] = hu[j, now + r : now + r + size, :] - DT * (
                    down - eta[j]
                )
                hv[j, new + r : new + r + size, :] = hv[j, now + r : now + r + size, :] - DT * (
                    right - eta[j]
                )
        for r in range(low, high, chunk):
            size = min(chunk, high - r)
            at_edge = lane[:size] == 0
            flux_y = [
                sy[j, 8 + r : 8 + r + size, :] * hv[j, new + r : new + r + size, :]
                for j in range(tiles)
            ]
            turned = [pltpu.roll(t, 1, 1) for t in flux_y]
            for j in range(tiles):
                flux_x = sx[j, 8 + r : 8 + r + size, :] * hu[j, new + r : new + r + size, :]
                flux_up = (
                    sx[j, 7 + r : 7 + r + size, :] * hu[j, new + r - 1 : new + r - 1 + size, :]
                )
                flux_left = jnp.where(at_edge, turned[(j - 1) % tiles], turned[j])
                eta = he[j, now + r : now + r + size, :] - DT * (
                    flux_x - flux_up + flux_y[j] - flux_left
                )
                if j == own:
                    eta = jnp.where(keep_cols[:size], eta, 0.0)
                if r >= rows + margin:
                    eta = jnp.where(keep_rows, eta, 0.0)
                elif r + size > rows + margin:
                    split = rows + margin - r
                    row = lax.broadcasted_iota(jnp.int32, (size, LANES), 0)
                    eta = jnp.where((row < split) | keep_rows, eta, 0.0)
                he[j, new + r : new + r + size, :] = eta

    last = steps * pitch + margin
    for out, hist in ((out_e, he), (out_u, hu), (out_v, hv)):
        for j in range(own):
            out[:, LANES * j : LANES * (j + 1)] = hist[j, last : last + rows, :]

    lane8 = lane_ids((8, LANES))
    count = cells.shape[1]

    def one_slot(k, kept):
        cell = cells[0, k]
        row = cell // cols
        col = cell % cols
        j = col // LANES
        shift = (k - col % LANES) % LANES
        out = []
        mine = lane8 == k
        for q, hist in enumerate((he, hu, hv)):
            for h in range(steps // 8):
                tile = hist[j, pl.ds((8 * h + 1) * pitch + margin + row, 8, stride=pitch), :]
                turned = pltpu.roll(tile, shift, 1)
                out.append(jnp.where(mine, turned, kept[q * (steps // 8) + h]))
        return tuple(out)

    zero = jnp.zeros((8, LANES), jnp.float32)
    kept = lax.fori_loop(0, count, one_slot, (zero,) * (3 * steps // 8), unroll=8)
    for t, tile in enumerate(kept):
        out_rec[8 * t : 8 * t + 8, :] = tile
    out_rec[3 * steps : 3 * steps + 8, :] = jnp.broadcast_to(ids[...].astype(jnp.float32), (8, LANES))


def place_kernel(base, rec, out, *, series, members):
    sources, _, slots = rec.shape
    gauges = members * GAUGE_DEV
    records = jnp.concatenate([rec[k, :series, :] for k in range(sources)], axis=1)
    one = records.astype(jnp.bfloat16)
    rest = records - one.astype(jnp.float32)
    two = rest.astype(jnp.bfloat16)
    three = (rest - two.astype(jnp.float32)).astype(jnp.bfloat16)
    terms = jnp.concatenate([one, two, three], axis=0)
    number = lax.broadcasted_iota(jnp.int32, (gauges, slots), 0)
    wanted = base[0] + (number // GAUGE_DEV) * (sources * GAUGE_DEV) + number % GAUGE_DEV
    wanted = wanted.astype(jnp.float32)
    picks = [
        (rec[k, series : series + 1, :] == wanted).astype(jnp.float32).astype(jnp.bfloat16)
        for k in range(sources)
    ]
    pick = jnp.concatenate(picks, axis=1)
    full = lax.dot_general(terms, pick, (((1,), (1,)), ((), ())), preferred_element_type=jnp.float32)
    dense = full[:series] + full[series : 2 * series] + full[2 * series :]
    half = series // 2
    low = lane_ids((half, LANES)) < GAUGE_DEV
    for t in range(gauges // LANES):
        tile = dense[:, LANES * t : LANES * (t + 1)]
        turned = pltpu.roll(tile, GAUGE_DEV, 1)
        out[2 * t] = jnp.where(low, tile[:half], turned[half:])
        out[2 * t + 1] = jnp.where(low, turned[:half], tile[half:])


def finish_kernel(parts, out, *, series):
    total = parts[0]
    for k in range(1, parts.shape[0]):
        total = total + parts[k]
    turned = pltpu.roll(total, GAUGE_DEV, 1)
    pad = jnp.zeros((LANES - series, LANES), jnp.float32)
    square = jnp.concatenate([total, turned, pad], axis=0)
    out[...] = jnp.transpose(square)[:GAUGE_DEV, :series]


def in_vmem(count):
    return [pl.BlockSpec(memory_space=pltpu.VMEM)] * count


def in_smem(count):
    return [pl.BlockSpec(memory_space=pltpu.SMEM)] * count


def f32(*shape):
    return jax.ShapeDtypeStruct(shape, jnp.float32)


def shards(surface, east, north, east_depth, north_depth, slot_gauge, slot_cell):
    rows, cols = surface.shape
    margin = STEPS
    series = 3 * STEPS
    n_gx, n_gy = lax.axis_size("gx"), lax.axis_size("gy")
    a, b = lax.axis_index("gx"), lax.axis_index("gy")
    fields = (surface, east, north, east_depth, north_depth)

    def shifted(tail, head, axis, count):
        from_before = lax.ppermute(tail, axis, [(i, i + 1) for i in range(count - 1)])
        from_after = lax.ppermute(head, axis, [(i + 1, i) for i in range(count - 1)])
        return from_before, from_after

    head_rows = jnp.concatenate([f[:margin] for f in fields], axis=0)
    tail_rows = jnp.concatenate([f[rows - margin :] for f in fields], axis=0)
    top, bot = shifted(tail_rows, head_rows, "gx", n_gx)

    height = rows + 2 * margin
    head, tail = pl.pallas_call(
        functools.partial(pack_columns_kernel, margin=margin),
        out_shape=(f32(height, LANES), f32(height, LANES)),
        in_specs=in_vmem(7),
        out_specs=tuple(in_vmem(2)),
        name="pack_columns",
    )(*fields, top, bot)
    from_left, from_right = shifted(tail, head, "gy", n_gy)

    tiles = cols // LANES + 1
    pitch = height + 8
    history = pltpu.VMEM((tiles, (STEPS + 1) * pitch, LANES), jnp.float32)
    depth = pltpu.VMEM((tiles, pitch, LANES), jnp.float32)
    edges = jnp.stack([a == n_gx - 1, b == n_gy - 1]).astype(jnp.int32)
    eta, u, v, rec = pl.pallas_call(
        functools.partial(steps_kernel, steps=STEPS),
        out_shape=(f32(rows, cols), f32(rows, cols), f32(rows, cols), f32(series + 8, LANES)),
        in_specs=in_smem(2) + in_vmem(10),
        out_specs=tuple(in_vmem(4)),
        scratch_shapes=[history, history, history, depth, depth],
        name="leapfrog",
    )(slot_cell, edges, slot_gauge, *fields, top, bot, from_left, from_right)

    near = [[QUAD * i + j for j in range(QUAD)] for i in range(n_gy // QUAD)]
    members = n_gy // QUAD
    far = [[i + QUAD * j for j in range(members)] for i in range(QUAD)]
    gathered = lax.all_gather(rec, "gy", axis_index_groups=near)
    base = (a * (n_gy * GAUGE_DEV) + (b % QUAD) * GAUGE_DEV).astype(jnp.int32).reshape(1)
    half = series // 2
    placed = pl.pallas_call(
        functools.partial(place_kernel, series=series, members=members),
        out_shape=f32(members, half, LANES),
        in_specs=in_smem(1) + in_vmem(1),
        out_specs=in_vmem(1)[0],
        name="place",
    )(base, gathered)
    arrived = lax.all_to_all(placed, "gy", 0, 0, axis_index_groups=far, tiled=True)
    out = pl.pallas_call(
        functools.partial(finish_kernel, series=series),
        out_shape=f32(GAUGE_DEV, series),
        in_specs=in_vmem(1),
        out_specs=in_vmem(1)[0],
        name="finish",
    )(arrived)
    return eta, u, v, out


def solution(mesh):
    block = P("gx", "gy")
    rows = P(("gx", "gy"), None)
    return jax.shard_map(
        shards,
        mesh=mesh,
        in_specs=(block,) * 5 + (rows, rows),
        out_specs=(block,) * 3 + (rows,),
        check_vma=False,
    )
```

time: 124 us -> 79.9 us (0.64); the launches traced: 122 us -> 79.4 us
  blocking collectives: 0 us -> 38.8 us
  matrix products: 36.1 us -> 0 us
  waiting for transfers between devices: 33.2 us -> 11.3 us
  starting transfers between devices: 30.1 us -> 9.33 us
  Pallas kernels: 0 us -> 14.1 us
  other arithmetic: 8.81 us -> 0.56 us
  local copies, waits for them, and re-layouts: 12 us -> 4.64 us
    dot_general x49 -> x0, matrix products: 36.1 us -> none  [the longest x48 34.4 us: sample_cells(): rows_taken = jnp.dot(row_pick, field, precision=lax.Precision.HIGHEST)]
    all_to_all x0 -> x1, blocking collectives: none -> 29.8 us  [shards(): lax.all_to_all(placed, 'gy', 0, 0, axis_index_groups=far, tiled=True)]
    all_to_all x1 -> x0, waiting for transfers between devices: 25.9 us -> none  [sent_and_summed(): lax.all_to_all(blocks, axis, split_axis=0, concat_axis=0, tiled=True)]
    all_to_all x1 -> x0, starting transfers between devices: 19.6 us -> none  [sent_and_summed(): lax.all_to_all(blocks, axis, split_axis=0, concat_axis=0, tiled=True)]
    pallas_call x0 -> x4, Pallas kernels: none -> 14.1 us  [the longest x1 8.36 us: shards(): pl.pallas_call(functools.partial(steps_kernel, steps=STEPS), out_shape=(f...]
    all_gather x0 -> x1, blocking collectives: none -> 8.99 us  [shards(): gathered = lax.all_gather(rec, 'gy', axis_index_groups=near)]
    mul x32 -> x0, other arithmetic: 5.74 us -> none  [the longest x16 3.23 us: advance_margin(): return (eta * inside, east, north)]
    slice x36 -> x0, local copies, waits for them, and re-layouts: 4.53 us -> none  [the longest x16 1.91 us: update_velocity(): eta_right = jnp.concatenate([eta[:, 1:], right], 1)]
  transfers between devices with their start and end apart: 5 -> 4, of which waited for: 4 -> 3; matrix products, arithmetic and copies ran while one was open for 2% -> 1% of each run, Pallas kernels for 0% -> 0%
where the time goes in v1:
time: 79.9 us; the launch traced here: 79.4 us
  blocking collectives  38.8 us (49%)
  Pallas kernels  14.1 us (18%)
  waiting for transfers between devices  11.3 us (14%)
  starting transfers between devices  9.33 us (12%)
  local copies, waits for them, and re-layouts  4.64 us (6%)
    all_to_all x1, blocking collectives, shards(): lax.all_to_all(placed, 'gy', 0, 0, axis_index_groups=far, tiled=True)  29.8 us
    all_gather x1, blocking collectives, shards(): gathered = lax.all_gather(rec, 'gy', axis_index_groups=near)  8.99 us
    pallas_call x1, Pallas kernels, shards(): pl.pallas_call(functools.partial(steps_kernel, steps=STEPS), out_shape=(f...  8.36 us
    ppermute x2, waiting for transfers between devices, shifted(): lax.ppermute(tail, axis, [(i, i + 1) for i in range(count - 1)])  6.23 us
    ppermute x2, starting transfers between devices, shifted(): lax.ppermute(head, axis, [(i + 1, i) for i in range(count - 1)])  6.13 us
    ppermute x2, waiting for transfers between devices, shifted(): lax.ppermute(head, axis, [(i + 1, i) for i in range(count - 1)])  5.12 us
    unnamed x21, local copies, waits for them, and re-layouts  4.63 us
    ppermute x2, starting transfers between devices, shifted(): lax.ppermute(tail, axis, [(i, i + 1) for i in range(count - 1)])  3.2 us
  transfers between devices with their start and end apart: 4, of which 3 were waited for; matrix products, arithmetic and copies ran while one was open for 1% of the time, Pallas kernels for 0%

profile of v1, /device:TPU:24, one launch (start us, length us, event | category | flops | bytes accessed | tf_op | source)
XLA Modules:
  0.0 79.4 jit_solution(13094277231917545156)
XLA Ops:
  0.6 0.0 copy-start
  0.6 0.0 copy-start.1
  0.7 0.8 %slice_dynamic-update-slice_fusion.4 = (f32[80,512]{1,0:T(8,128)S(1)}, f32[80,512]{1,0:T(8,128)S(1)}) fusion(f32[64,512]{1,0:T(8,128)} %e.3), kind=kLoop, calls=%fused_computation.4 | loop fusion | bytes 131072
  1.5 0.1 copy-done
  1.5 0.0 copy-start.2
  1.5 0.1 copy-done.1
  1.6 0.0 copy-start.3
  1.6 0.8 %copy-done.2 = f32[64,512]{1,0:T(8,128)S(1)} copy-done((f32[64,512]{1,0:T(8,128)S(1)}, f32[64,512]{1,0:T(8,128)}, u32[]{:S(2)}) %copy-start.2) | copy-done | bytes 131096
  2.5 0.1 copy-done.3
  2.6 4.8 %collective-permute-start.1 = (f32[80,512]{1,0:T(8,128)S(1)}, f32[80,512]{1,0:T(8,128)S(1)}, u32[]{:S(2)}, u32[]{:S(2)}) collective-permute-start(f32[80,512]{1,0:T(8,128)S(1)} %get-tuple-element.20), channel_id=1, source_target_pairs={{32,0},{64,32},{96,64},{128,96},{160,128},{192,160},{224,192},{256... | collective-permute-start | bytes 491528 | tf_op jit(solution)/shard_map/ppermute | solution.py:218
  7.4 1.9 %collective-permute-start = (f32[80,512]{1,0:T(8,128)S(1)}, f32[80,512]{1,0:T(8,128)S(1)}, u32[]{:S(2)}, u32[]{:S(2)}) collective-permute-start(f32[80,512]{1,0:T(8,128)S(1)} %get-tuple-element.21), channel_id=1, source_target_pairs={{0,32},{32,64},{64,96},{96,128},{128,160},{160,192},{192,224},{224... | collective-permute-start | bytes 491528 | tf_op jit(solution)/shard_map/ppermute | solution.py:217
  9.3 1.5 %collective-permute-done.1.bot = f32[80,512]{1,0:T(8,128)S(1)} collective-permute-done((f32[80,512]{1,0:T(8,128)S(1)}, f32[80,512]{1,0:T(8,128)S(1)}, u32[]{:S(2)}, u32[]{:S(2)}) %collective-permute-start.1) | collective-permute-done | bytes 163872 | tf_op jit(solution)/shard_map/ppermute | solution.py:218
  10.8 0.0 copy-start.4
  10.8 6.2 %collective-permute-done.top = f32[80,512]{1,0:T(8,128)S(1)} collective-permute-done((f32[80,512]{1,0:T(8,128)S(1)}, f32[80,512]{1,0:T(8,128)S(1)}, u32[]{:S(2)}, u32[]{:S(2)}) %collective-permute-start) | collective-permute-done | bytes 163872 | tf_op jit(solution)/shard_map/ppermute | solution.py:217
  17.1 0.0 copy-done.4
  17.1 0.0 copy-start.5
  17.1 0.7 copy-done.5
  17.7 2.1 %pack_columns.1 = (f32[96,128]{1,0:T(8,128)}, f32[96,128]{1,0:T(8,128)}) custom-call(f32[64,512]{1,0:T(8,128)} %e.3, f32[64,512]{1,0:T(8,128)} %u.3, f32[64,512]{1,0:T(8,128)} %v.3, f32[64,512]{1,0:T(8,128)} %dx.3, f32[64,512]{1,0:T(8,128)} %dy.3, f32[80,512]{1,0:T(8,128)} %copy-done.5, f32[80,512]{1,0:T(8,128)} %copy-done.4), custom_call_target="tpu_custom_call" | custom-call | tf_op jit(solution)/shard_map/pack_columns/pallas_call | solution.py:226
  19.8 1.3 %collective-permute-start.2 = (f32[96,128]{1,0:T(8,128)}, f32[96,128]{1,0:T(8,128)S(1)}, u32[]{:S(2)}, u32[]{:S(2)}) collective-permute-start(f32[96,128]{1,0:T(8,128)} %get-tuple-element.10), channel_id=1, source_target_pairs={{0,1},{1,2},{2,3},{3,4},{4,5},{5,6},{6,7},{7,8},{8,9},{9,10},{10,1... | collective-permute-start | bytes 147464 | tf_op jit(solution)/shard_map/ppermute | solution.py:217
  21.1 1.3 %collective-permute-start.3 = (f32[96,128]{1,0:T(8,128)}, f32[96,128]{1,0:T(8,128)S(1)}, u32[]{:S(2)}, u32[]{:S(2)}) collective-permute-start(f32[96,128]{1,0:T(8,128)} %get-tuple-element.11), channel_id=1, source_target_pairs={{1,0},{2,1},{3,2},{4,3},{5,4},{6,5},{7,6},{8,7},{9,8},{10,9},{11,1... | collective-permute-start | bytes 147464 | tf_op jit(solution)/shard_map/ppermute | solution.py:218
  22.4 0.6 add_convert_fusion.edges
  23.0 0.0 collective-permute-done.2.from_left
  23.0 3.6 %collective-permute-done.3.from_right = f32[96,128]{1,0:T(8,128)S(1)} collective-permute-done((f32[96,128]{1,0:T(8,128)}, f32[96,128]{1,0:T(8,128)S(1)}, u32[]{:S(2)}, u32[]{:S(2)}) %collective-permute-start.3) | collective-permute-done | bytes 49184 | tf_op jit(solution)/shard_map/ppermute | solution.py:218
  26.6 0.0 copy-done.6
  26.6 0.0 copy-start.7
  26.6 0.6 copy-done.7
  27.2 8.4 %leapfrog.1 = (f32[64,512]{1,0:T(8,128)}, f32[64,512]{1,0:T(8,128)}, f32[64,512]{1,0:T(8,128)}, f32[56,128]{1,0:T(8,128)}) custom-call(s32[1,128]{1,0:T(1,128)} %cells.1, s32[2]{0:T(128)} %add_convert_fusion.edges, s32[1,128]{1,0:T(1,128)} %ids.1, f32[64,512]{1,0:T(8,128)} %e.3, f32[64,512]{1,0:T(8,128)} %u.3, f32[64,512]{1,0:T(8,128)} %v.3, f32[64,512]{1,0:T(8,128)} %dx.3, ...), custom_call_target="tpu_custom_call" | custom-call | tf_op jit(solution)/shard_map/leapfrog/pallas_call | solution.py:240
  35.6 9.0 %all-gather = f32[224,128]{1,0:T(8,128)} all-gather(f32[56,128]{1,0:T(8,128)} %get-tuple-element.15), channel_id=2, replica_groups={{0,1,2,3},{4,5,6,7},{8,9,10,11},{12,13,14,15},{16,17,18,19},{20,21,22,2..., dimensions={0}, use_global_device_ids=true | all-gather | bytes 143360 | tf_op jit(solution)/shard_map/all_gather | solution.py:252
  44.6 2.0 %place.1 = f32[8,24,128]{2,1,0:T(8,128)} custom-call(s32[1]{0:T(128)} %bitcast.2.base, f32[4,56,128]{2,1,0:T(8,128)} %bitcast.4), custom_call_target="tpu_custom_call" | custom-call | tf_op jit(solution)/shard_map/place/pallas_call | solution.py:255
  46.5 29.8 %all_to_all.5.parts = f32[8,24,128]{2,1,0:T(8,128)} all-to-all(f32[8,24,128]{2,1,0:T(8,128)} %place.1), channel_id=1, replica_groups={{0,4,8,12,16,20,24,28},{1,5,9,13,17,21,25,29},{2,6,10,14,18,22,26,30},{..., dimensions={0} | all-to-all | bytes 196608 | tf_op jit(solution)/shard_map/all_to_all | solution.py:262
  76.3 1.7 %finish.1 = f32[64,48]{1,0:T(8,128)} custom-call(f32[8,24,128]{2,1,0:T(8,128)} %all_to_all.5.parts), custom_call_target="tpu_custom_call" | custom-call | tf_op jit(solution)/shard_map/finish/pallas_call | solution.py:263
  78.0 1.4 %copy.11 = f32[64,48]{0,1:T(8,128)} copy(f32[64,48]{1,0:T(8,128)} %finish.1) | data formatting | bytes 24576
  (5 shorter events, 0.0 us)
Async XLA Ops:
  0.6 0.9 %copy-start = (f32[64,512]{1,0:T(8,128)S(1)}, f32[64,512]{1,0:T(8,128)}, u32[]{:S(2)}) copy-start(f32[64,512]{1,0:T(8,128)} %u.3) | copy-start | bytes 393220
  0.6 1.0 %copy-start.1 = (f32[64,512]{1,0:T(8,128)S(1)}, f32[64,512]{1,0:T(8,128)}, u32[]{:S(2)}) copy-start(f32[64,512]{1,0:T(8,128)} %v.3) | copy-start | bytes 393220
  1.5 0.9 %copy-start.2 = (f32[64,512]{1,0:T(8,128)S(1)}, f32[64,512]{1,0:T(8,128)}, u32[]{:S(2)}) copy-start(f32[64,512]{1,0:T(8,128)} %dx.3) | copy-start | bytes 393220
  1.6 0.9 %copy-start.3 = (f32[64,512]{1,0:T(8,128)S(1)}, f32[64,512]{1,0:T(8,128)}, u32[]{:S(2)}) copy-start(f32[64,512]{1,0:T(8,128)} %dy.3) | copy-start | bytes 393220
  2.6 8.3 %collective-permute-start.1 = (f32[80,512]{1,0:T(8,128)S(1)}, f32[80,512]{1,0:T(8,128)S(1)}, u32[]{:S(2)}, u32[]{:S(2)}) collective-permute-start(f32[80,512]{1,0:T(8,128)S(1)} %get-tuple-element.20), channel_id=1, source_target_pairs={{32,0},{64,32},{96,64},{128,96},{160,128},{192,160},{224,192},{256... | collective-permute-start | bytes 491528 | tf_op jit(solution)/shard_map/ppermute | solution.py:218
  7.4 9.7 %collective-permute-start = (f32[80,512]{1,0:T(8,128)S(1)}, f32[80,512]{1,0:T(8,128)S(1)}, u32[]{:S(2)}, u32[]{:S(2)}) collective-permute-start(f32[80,512]{1,0:T(8,128)S(1)} %get-tuple-element.21), channel_id=1, source_target_pairs={{0,32},{32,64},{64,96},{96,128},{128,160},{160,192},{192,224},{224... | collective-permute-start | bytes 491528 | tf_op jit(solution)/shard_map/ppermute | solution.py:217
  10.8 6.2 %copy-start.4 = (f32[80,512]{1,0:T(8,128)}, f32[80,512]{1,0:T(8,128)S(1)}, u32[]{:S(2)}) copy-start(f32[80,512]{1,0:T(8,128)S(1)} %collective-permute-done.1.bot) | copy-start | bytes 491524
  17.1 0.7 copy-start.5
  19.8 3.2 %collective-permute-start.2 = (f32[96,128]{1,0:T(8,128)}, f32[96,128]{1,0:T(8,128)S(1)}, u32[]{:S(2)}, u32[]{:S(2)}) collective-permute-start(f32[96,128]{1,0:T(8,128)} %get-tuple-element.10), channel_id=1, source_target_pairs={{0,1},{1,2},{2,3},{3,4},{4,5},{5,6},{6,7},{7,8},{8,9},{9,10},{10,1... | collective-permute-start | bytes 147464 | tf_op jit(solution)/shard_map/ppermute | solution.py:217
  21.1 5.5 %collective-permute-start.3 = (f32[96,128]{1,0:T(8,128)}, f32[96,128]{1,0:T(8,128)S(1)}, u32[]{:S(2)}, u32[]{:S(2)}) collective-permute-start(f32[96,128]{1,0:T(8,128)} %get-tuple-element.11), channel_id=1, source_target_pairs={{1,0},{2,1},{3,2},{4,3},{5,4},{6,5},{7,6},{8,7},{9,8},{10,9},{11,1... | collective-permute-start | bytes 147464 | tf_op jit(solution)/shard_map/ppermute | solution.py:218
  23.0 3.6 %copy-start.6 = (f32[96,128]{1,0:T(8,128)}, f32[96,128]{1,0:T(8,128)S(1)}, u32[]{:S(2)}) copy-start(f32[96,128]{1,0:T(8,128)S(1)} %collective-permute-done.2.from_left) | copy-start | bytes 147460
  26.6 0.6 copy-start.7

commit v2 on v1

v2 whole, which is shorter than its diff:
```python
import functools

import jax
import jax.numpy as jnp
from jax import lax
from jax.experimental import pallas as pl
from jax.experimental.pallas import tpu as pltpu
from jax.sharding import PartitionSpec as P

STEPS = 16
GAUGE_DEV = 64
QUAD = 4
LANES = 128
DT = 0.45
MIB = 1 << 20


def lane_ids(shape):
    return lax.broadcasted_iota(jnp.int32, shape, 1)


def pack_columns_kernel(e, u, v, dx, dy, top, bot, head, tail, *, margin):
    rows, cols = e.shape
    lane = lane_ids((margin, LANES))
    last = cols - LANES
    fields = (e, u, v, dx, dy)
    for r in range(0, rows + 2 * margin, margin):
        out_head = jnp.zeros((margin, LANES), jnp.float32)
        out_tail = jnp.zeros((margin, LANES), jnp.float32)
        for f, ref in enumerate(fields):
            if r == 0:
                src, at = top, f * margin
            elif r == rows + margin:
                src, at = bot, f * margin
            else:
                src, at = ref, r - margin
            first = src[at : at + margin, :LANES]
            final = src[at : at + margin, last:]
            mine = (lane >= margin * f) & (lane < margin * (f + 1))
            if f:
                first = pltpu.roll(first, margin * f, 1)
            final = pltpu.roll(final, (margin * f + margin) % LANES, 1)
            out_head = jnp.where(mine, first, out_head)
            out_tail = jnp.where(mine, final, out_tail)
        head[r : r + margin, :] = out_head
        tail[r : r + margin, :] = out_tail


def pack_rows_kernel(e, u, v, dx, dy, head, tail, sems, *, margin):
    rows = e.shape[0]
    copies = []
    for f, ref in enumerate((e, u, v, dx, dy)):
        place = pl.ds(margin * f, margin)
        copies.append(pltpu.make_async_copy(ref.at[pl.ds(0, margin), :], head.at[place, :], sems.at[f]))
        copies.append(
            pltpu.make_async_copy(ref.at[pl.ds(rows - margin, margin), :], tail.at[place, :], sems.at[5 + f])
        )
    for copy in copies:
        copy.start()
    for copy in copies:
        copy.wait()


def steps_kernel(
    cells_in, place_x, place_y, ids_in, e, u, v, dx, dy, top, bot, from_left, from_right,
    out_e, out_u, out_v, out_rec, he, hu, hv, sx, sy, cells, ids, staged, list_sems, out_sems,
    *, steps, last_x, last_y,
):
    rows, cols = e.shape
    margin = steps
    own = cols // LANES
    tiles = own + 1
    height = rows + 2 * margin
    pitch = height + 8
    chunk = 16
    lane = lane_ids((chunk, LANES))
    lists = [
        pltpu.make_async_copy(cells_in, cells, list_sems.at[0]),
        pltpu.make_async_copy(ids_in, ids, list_sems.at[1]),
    ]
    for copy in lists:
        copy.start()

    for f, (ref, dst, factor) in enumerate(
        ((e, he, DT), (u, hu, None), (v, hv, None), (dx, sx, DT * DT), (dy, sy, DT * DT))
    ):
        def scaled(value):
            return value if factor is None else value * factor

        for j in range(own):
            cut = slice(LANES * j, LANES * (j + 1))
            dst[j, :margin, :] = scaled(top[f * margin : (f + 1) * margin, cut])
            dst[j, margin : margin + rows, :] = scaled(ref[:, cut])
            dst[j, margin + rows : height, :] = scaled(bot[f * margin : (f + 1) * margin, cut])
        for r in range(0, height, chunk):
            right = from_right[r : r + chunk, :]
            left = from_left[r : r + chunk, :]
            if f:
                right = pltpu.roll(right, LANES - margin * f, 1)
            left = pltpu.roll(left, (LANES - margin - margin * f) % LANES, 1)
            tile = jnp.where(
                lane < margin, right, jnp.where(lane >= LANES - margin, left, jnp.zeros_like(left))
            )
            dst[own, r : r + chunk, :] = scaled(tile)

    size = 8
    lane8 = lane_ids((size, LANES))
    row8 = lax.broadcasted_iota(jnp.int32, (size, LANES), 0)
    first_lane, final_lane, final_row = lane8 == 0, lane8 == LANES - 1, row8 == size - 1
    keep_rows = place_x[0] != last_x
    keep_cols = (lane8 >= LANES // 2) | (place_y[0] != last_y)

    for s in range(steps):
        low = (s // size) * size
        now, new = s * pitch, (s + 1) * pitch
        flux_before = [None] * tiles
        for r in range(low, height - low, size):
            eta = [he[j, now + r : now + r + size, :] for j in range(tiles)]
            flux_y = []
            for j in range(tiles):
                right = pltpu.roll(jnp.where(first_lane, eta[(j + 1) % tiles], eta[j]), LANES - 1, 1)
                north = hv[j, now + r : now + r + size, :] - (right - eta[j])
                hv[j, new + r : new + r + size, :] = north
                flux_y.append(sy[j, r : r + size, :] * north)
            for j in range(tiles):
                down = he[j, now + r + 1 : now + r + 1 + size, :]
                east = hu[j, now + r : now + r + size, :] - (down - eta[j])
                hu[j, new + r : new + r + size, :] = east
                flux_x = sx[j, r : r + size, :] * east
                above = flux_x if flux_before[j] is None else flux_before[j]
                flux_up = pltpu.roll(jnp.where(final_row, above, flux_x), 1, 0)
                flux_before[j] = flux_x
                flux_left = pltpu.roll(jnp.where(final_lane, flux_y[(j - 1) % tiles], flux_y[j]), 1, 1)
                after = eta[j] - ((flux_x - flux_up) + (flux_y[j] - flux_left))
                if j == own:
                    after = jnp.where(keep_cols, after, 0.0)
                if r >= rows + margin:
                    after = jnp.where(keep_rows, after, 0.0)
                he[j, new + r : new + r + size, :] = after

    last = steps * pitch + margin
    outs = []
    for j in range(own):
        cut = pl.ds(LANES * j, LANES)
        outs.append(pltpu.make_async_copy(hu.at[j, pl.ds(last, rows), :], out_u.at[:, cut], out_sems.at[j]))
        outs.append(
            pltpu.make_async_copy(hv.at[j, pl.ds(last, rows), :], out_v.at[:, cut], out_sems.at[own + j])
        )
    outs.append(pltpu.make_async_copy(staged, out_e, out_sems.at[2 * own]))
    for copy in outs[:-1]:
        copy.start()
    for j in range(own):
        staged[:, LANES * j : LANES * (j + 1)] = he[j, last : last + rows, :] * (1.0 / DT)
    outs[-1].start()
    for copy in lists:
        copy.wait()

    count = cells.shape[1]
    groups = steps // size

    def one_slot(k, kept):
        cell = cells[0, k]
        row = cell >> (cols.bit_length() - 1)
        col = cell & (cols - 1)
        j = col >> (LANES.bit_length() - 1)
        shift = (k - col) & (LANES - 1)
        out = []
        mine = lane8 == k
        for q, hist in enumerate((he, hu, hv)):
            for h in range(groups):
                tile = hist[j, pl.ds((size * h + 1) * pitch + margin + row, size, stride=pitch), :]
                turned = pltpu.roll(tile, shift, 1)
                out.append(jnp.where(mine, turned, kept[q * groups + h]))
        return tuple(out)

    zero = jnp.zeros((size, LANES), jnp.float32)
    kept = lax.fori_loop(0, count, one_slot, (zero,) * (3 * groups), unroll=32)
    for t, tile in enumerate(kept):
        out_rec[size * t : size * (t + 1), :] = tile * (1.0 / DT) if t < groups else tile
    out_rec[3 * steps : 3 * steps + 8, :] = jnp.broadcast_to(ids[...].astype(jnp.float32), (8, LANES))
    for copy in outs:
        copy.wait()


def place_kernel(base, rec, out, *, series, members):
    sources, _, slots = rec.shape
    gauges = members * GAUGE_DEV
    records = jnp.concatenate([rec[k, :series, :] for k in range(sources)], axis=1)
    one = records.astype(jnp.bfloat16)
    rest = records - one.astype(jnp.float32)
    two = rest.astype(jnp.bfloat16)
    three = (rest - two.astype(jnp.float32)).astype(jnp.bfloat16)
    terms = jnp.concatenate([one, two, three], axis=0)
    number = lax.broadcasted_iota(jnp.int32, (gauges, slots), 0)
    wanted = base[0] + (number // GAUGE_DEV) * (sources * GAUGE_DEV) + number % GAUGE_DEV
    wanted = wanted.astype(jnp.float32)
    picks = [
        (rec[k, series : series + 1, :] == wanted).astype(jnp.float32).astype(jnp.bfloat16)
        for k in range(sources)
    ]
    pick = jnp.concatenate(picks, axis=1)
    full = lax.dot_general(terms, pick, (((1,), (1,)), ((), ())), preferred_element_type=jnp.float32)
    dense = full[:series] + full[series : 2 * series] + full[2 * series :]
    half = series // 2
    low = lane_ids((half, LANES)) < GAUGE_DEV
    for t in range(gauges // LANES):
        tile = dense[:, LANES * t : LANES * (t + 1)]
        turned = pltpu.roll(tile, GAUGE_DEV, 1)
        out[2 * t] = jnp.where(low, tile[:half], turned[half:])
        out[2 * t + 1] = jnp.where(low, turned[:half], tile[half:])


def finish_kernel(parts, out, *, series):
    total = parts[0]
    for k in range(1, parts.shape[0]):
        total = total + parts[k]
    turned = pltpu.roll(total, GAUGE_DEV, 1)
    out[: series // 2, :] = total[:, :GAUGE_DEV]
    out[series // 2 :, :] = turned[:, :GAUGE_DEV]


def in_vmem(count):
    return [pl.BlockSpec(memory_space=pltpu.VMEM)] * count


def in_smem(count):
    return [pl.BlockSpec(memory_space=pltpu.SMEM)] * count


def f32(*shape):
    return jax.ShapeDtypeStruct(shape, jnp.float32)


def shards(surface, east, north, east_depth, north_depth, slot_gauge, slot_cell):
    rows, cols = surface.shape
    margin = STEPS
    series = 3 * STEPS
    n_gx, n_gy = lax.axis_size("gx"), lax.axis_size("gy")
    a, b = lax.axis_index("gx"), lax.axis_index("gy")
    fields = (surface, east, north, east_depth, north_depth)

    def shifted(tail, head, axis, count):
        from_before = lax.ppermute(tail, axis, [(i, i + 1) for i in range(count - 1)])
        from_after = lax.ppermute(head, axis, [(i + 1, i) for i in range(count - 1)])
        return from_before, from_after

    whole = pl.BlockSpec(memory_space=pltpu.HBM)
    head_rows, tail_rows = pl.pallas_call(
        functools.partial(pack_rows_kernel, margin=margin),
        out_shape=(f32(5 * margin, cols), f32(5 * margin, cols)),
        in_specs=[whole] * 5,
        out_specs=tuple(in_vmem(2)),
        scratch_shapes=[pltpu.SemaphoreType.DMA((10,))],
        compiler_params=pltpu.CompilerParams(vmem_limit_bytes=4 * MIB),
        name="pack_rows",
    )(*(pltpu.with_memory_space_constraint(f, pltpu.HBM) for f in fields))
    top, bot = shifted(tail_rows, head_rows, "gx", n_gx)

    height = rows + 2 * margin
    head, tail = pl.pallas_call(
        functools.partial(pack_columns_kernel, margin=margin),
        out_shape=(f32(height, LANES), f32(height, LANES)),
        in_specs=in_vmem(7),
        out_specs=tuple(in_vmem(2)),
        compiler_params=pltpu.CompilerParams(vmem_limit_bytes=4 * MIB),
        name="pack_columns",
    )(*fields, top, bot)
    from_left, from_right = shifted(tail, head, "gy", n_gy)

    tiles = cols // LANES + 1
    pitch = height + 8
    history = pltpu.VMEM((tiles, (STEPS + 1) * pitch, LANES), jnp.float32)
    depth = pltpu.VMEM((tiles, height, LANES), jnp.float32)
    eta, u, v, rec = pl.pallas_call(
        functools.partial(steps_kernel, steps=STEPS, last_x=n_gx - 1, last_y=n_gy - 1),
        out_shape=(f32(rows, cols), f32(rows, cols), f32(rows, cols), f32(series + 8, LANES)),
        in_specs=[whole] + in_smem(2) + [whole] + in_vmem(9),
        out_specs=(whole,) * 3 + tuple(in_vmem(1)),
        scratch_shapes=[
            history, history, history, depth, depth,
            pltpu.SMEM(slot_cell.shape, jnp.int32),
            pltpu.VMEM(slot_gauge.shape, jnp.int32),
            pltpu.VMEM((rows, cols), jnp.float32),
            pltpu.SemaphoreType.DMA((2,)),
            pltpu.SemaphoreType.DMA((2 * tiles - 1,)),
        ],
        compiler_params=pltpu.CompilerParams(vmem_limit_bytes=24 * MIB),
        name="leapfrog",
    )(
        pltpu.with_memory_space_constraint(slot_cell, pltpu.HBM),
        a.astype(jnp.int32).reshape(1),
        b.astype(jnp.int32).reshape(1),
        pltpu.with_memory_space_constraint(slot_gauge, pltpu.HBM),
        *fields, top, bot, from_left, from_right,
    )

    near = [[QUAD * i + j for j in range(QUAD)] for i in range(n_gy // QUAD)]
    members = n_gy // QUAD
    far = [[i + QUAD * j for j in range(members)] for i in range(QUAD)]
    gathered = lax.all_gather(rec, "gy", axis_index_groups=near)
    base = (a * (n_gy * GAUGE_DEV) + (b % QUAD) * GAUGE_DEV).astype(jnp.int32).reshape(1)
    half = series // 2
    placed = pl.pallas_call(
        functools.partial(place_kernel, series=series, members=members),
        out_shape=f32(members, half, LANES),
        in_specs=in_smem(1) + in_vmem(1),
        out_specs=in_vmem(1)[0],
        compiler_params=pltpu.CompilerParams(vmem_limit_bytes=8 * MIB),
        name="place",
    )(base, gathered)
    arrived = lax.all_to_all(placed, "gy", 0, 0, axis_index_groups=far, tiled=True)
    out = pl.pallas_call(
        functools.partial(finish_kernel, series=series),
        out_shape=f32(series, GAUGE_DEV),
        in_specs=in_vmem(1),
        out_specs=in_vmem(1)[0],
        compiler_params=pltpu.CompilerParams(vmem_limit_bytes=4 * MIB),
        name="finish",
    )(arrived)
    return eta, u, v, out.T


def solution(mesh):
    block = P("gx", "gy")
    rows = P(("gx", "gy"), None)
    return jax.shard_map(
        shards,
        mesh=mesh,
        in_specs=(block,) * 5 + (rows, rows),
        out_specs=(block,) * 3 + (rows,),
        check_vma=False,
    )
```

time: 79.9 us -> 67.1 us (0.84)
  the two profiles are of different devices: /device:TPU:24 before, /device:TPU:14 now
where the time goes in v2:
time: 67.1 us; the launch traced here: 66.8 us
  blocking collectives  36.8 us (55%)
  waiting for transfers between devices  11.2 us (17%)
  Pallas kernels  9.64 us (14%)
  starting transfers between devices  8.43 us (13%)
  between operations  0.78 us (1%)
    all_to_all x1, blocking collectives, shards(): lax.all_to_all(placed, 'gy', 0, 0, axis_index_groups=far, tiled=True)  28.8 us
    ppermute x2, waiting for transfers between devices, shifted(): lax.ppermute(head, axis, [(i + 1, i) for i in range(count - 1)])  9.19 us
    all_gather x1, blocking collectives, shards(): gathered = lax.all_gather(rec, 'gy', axis_index_groups=near)  8.03 us
    pallas_call x1, Pallas kernels, shards(): pl.pallas_call(functools.partial(steps_kernel, steps=STEPS, last_x=n_gx -...  7.31 us
    ppermute x2, starting transfers between devices, shifted(): lax.ppermute(tail, axis, [(i, i + 1) for i in range(count - 1)])  4.69 us
    ppermute x2, starting transfers between devices, shifted(): lax.ppermute(head, axis, [(i + 1, i) for i in range(count - 1)])  3.74 us
    ppermute x2, waiting for transfers between devices, shifted(): lax.ppermute(tail, axis, [(i, i + 1) for i in range(count - 1)])  1.98 us
  transfers between devices with their start and end apart: 4, of which 3 were waited for; matrix products, arithmetic and copies ran while one was open for 0% of the time, Pallas kernels for 0%

profile of v2, /device:TPU:14, one launch (start us, length us, event | category | flops | bytes accessed | tf_op | source)
XLA Modules:
  0.0 66.8 jit_solution(13362292713530481782)
XLA Ops:
  0.6 0.0 copy-start
  0.6 0.0 copy-start.1
  0.7 0.0 copy-start.2
  0.7 0.0 copy-start.3
  0.7 0.0 copy-start.4
  0.7 1.1 %pack_rows.1 = (f32[80,512]{1,0:T(8,128)S(1)}, f32[80,512]{1,0:T(8,128)S(1)}) custom-call(f32[64,512]{1,0:T(8,128)} %e.5, f32[64,512]{1,0:T(8,128)} %u.5, f32[64,512]{1,0:T(8,128)} %v.5, f32[64,512]{1,0:T(8,128)} %dx.5, f32[64,512]{1,0:T(8,128)} %dy.5), custom_call_target="tpu_custom_call" | custom-call | tf_op jit(solution)/shard_map/pack_rows/pallas_call | solution.py:248
  1.7 3.4 %collective-permute-start = (f32[80,512]{1,0:T(8,128)S(1)}, f32[80,512]{1,0:T(8,128)S(1)}, u32[]{:S(2)}, u32[]{:S(2)}) collective-permute-start(f32[80,512]{1,0:T(8,128)S(1)} %get-tuple-element.12), channel_id=1, source_target_pairs={{0,32},{32,64},{64,96},{96,128},{128,160},{160,192},{192,224},{224... | collective-permute-start | bytes 491528 | tf_op jit(solution)/shard_map/ppermute | solution.py:243
  5.2 2.4 %collective-permute-start.1 = (f32[80,512]{1,0:T(8,128)S(1)}, f32[80,512]{1,0:T(8,128)S(1)}, u32[]{:S(2)}, u32[]{:S(2)}) collective-permute-start(f32[80,512]{1,0:T(8,128)S(1)} %get-tuple-element.13), channel_id=1, source_target_pairs={{32,0},{64,32},{96,64},{128,96},{160,128},{192,160},{224,192},{256... | collective-permute-start | bytes 491528 | tf_op jit(solution)/shard_map/ppermute | solution.py:244
  7.6 2.0 %collective-permute-done.top = f32[80,512]{1,0:T(8,128)S(1)} collective-permute-done((f32[80,512]{1,0:T(8,128)S(1)}, f32[80,512]{1,0:T(8,128)S(1)}, u32[]{:S(2)}, u32[]{:S(2)}) %collective-permute-start) | collective-permute-done | bytes 163872 | tf_op jit(solution)/shard_map/ppermute | solution.py:243
  9.6 5.2 %collective-permute-done.1.bot = f32[80,512]{1,0:T(8,128)S(1)} collective-permute-done((f32[80,512]{1,0:T(8,128)S(1)}, f32[80,512]{1,0:T(8,128)S(1)}, u32[]{:S(2)}, u32[]{:S(2)}) %collective-permute-start.1) | collective-permute-done | bytes 163872 | tf_op jit(solution)/shard_map/ppermute | solution.py:244
  14.8 0.0 copy-done
  14.8 0.0 copy-done.1
  14.8 0.0 copy-done.2
  14.8 0.0 copy-done.3
  14.8 0.0 copy-done.4
  14.8 0.2 pack_columns.1
  15.0 1.3 %collective-permute-start.2 = (f32[96,128]{1,0:T(8,128)S(1)}, f32[96,128]{1,0:T(8,128)S(1)}, u32[]{:S(2)}, u32[]{:S(2)}) collective-permute-start(f32[96,128]{1,0:T(8,128)S(1)} %get-tuple-element.14), channel_id=1, source_target_pairs={{0,1},{1,2},{2,3},{3,4},{4,5},{5,6},{6,7},{7,8},{8,9},{9,10},{10,1... | collective-permute-start | bytes 147464 | tf_op jit(solution)/shard_map/ppermute | solution.py:243
  16.3 1.3 %collective-permute-start.3 = (f32[96,128]{1,0:T(8,128)S(1)}, f32[96,128]{1,0:T(8,128)S(1)}, u32[]{:S(2)}, u32[]{:S(2)}) collective-permute-start(f32[96,128]{1,0:T(8,128)S(1)} %get-tuple-element.15), channel_id=1, source_target_pairs={{1,0},{2,1},{3,2},{4,3},{5,4},{6,5},{7,6},{8,7},{9,8},{10,9},{11,1... | collective-permute-start | bytes 147464 | tf_op jit(solution)/shard_map/ppermute | solution.py:244
  17.6 0.0 collective-permute-done.2.from_left
  17.7 4.0 %collective-permute-done.3.from_right = f32[96,128]{1,0:T(8,128)S(1)} collective-permute-done((f32[96,128]{1,0:T(8,128)S(1)}, f32[96,128]{1,0:T(8,128)S(1)}, u32[]{:S(2)}, u32[]{:S(2)}) %collective-permute-start.3) | collective-permute-done | bytes 49184 | tf_op jit(solution)/shard_map/ppermute | solution.py:244
  21.6 7.3 %leapfrog.1 = (f32[64,512]{1,0:T(8,128)}, f32[64,512]{1,0:T(8,128)}, f32[64,512]{1,0:T(8,128)}, f32[56,128]{1,0:T(8,128)S(1)}) custom-call(s32[1,128]{1,0:T(1,128)} %cells_in.1, s32[1]{0:T(128)} %bitcast.place_x, s32[1]{0:T(128)} %bitcast.1.place_y, s32[1,128]{1,0:T(1,128)} %ids_in.1, f32[64,512]{1,0:T(8,128)S(1)} %copy-done, f32[64,512]{1,0:T(8,128)S(1)} %copy-done.1, ...), custom_call_target="tpu_custom_call" | custom-call | tf_op jit(solution)/shard_map/leapfrog/pallas_call | solution.py:274
  28.9 8.0 %all-gather = f32[224,128]{1,0:T(8,128)S(1)} all-gather(f32[56,128]{1,0:T(8,128)S(1)} %get-tuple-element.19), channel_id=2, replica_groups={{0,1,2,3},{4,5,6,7},{8,9,10,11},{12,13,14,15},{16,17,18,19},{20,21,22,2..., dimensions={0}, use_global_device_ids=true | all-gather | bytes 143360 | tf_op jit(solution)/shard_map/all_gather | solution.py:300
  37.0 0.4 place.1
  37.4 28.8 %all_to_all.5.parts = f32[8,24,128]{2,1,0:T(8,128)S(1)} all-to-all(f32[8,24,128]{2,1,0:T(8,128)S(1)} %place.1), channel_id=1, replica_groups={{0,4,8,12,16,20,24,28},{1,5,9,13,17,21,25,29},{2,6,10,14,18,22,26,30},{..., dimensions={0} | all-to-all | bytes 196608 | tf_op jit(solution)/shard_map/all_to_all | solution.py:311
  66.1 0.7 %finish.1 = f32[48,64]{1,0:T(8,128)} custom-call(f32[8,24,128]{2,1,0:T(8,128)S(1)} %all_to_all.5.parts), custom_call_target="tpu_custom_call" | custom-call | tf_op jit(solution)/shard_map/finish/pallas_call | solution.py:312
Async XLA Ops:
  0.6 14.2 %copy-start = (f32[64,512]{1,0:T(8,128)S(1)}, f32[64,512]{1,0:T(8,128)}, u32[]{:S(2)}) copy-start(f32[64,512]{1,0:T(8,128)} %e.5) | copy-start | bytes 393220
  0.6 14.2 %copy-start.1 = (f32[64,512]{1,0:T(8,128)S(1)}, f32[64,512]{1,0:T(8,128)}, u32[]{:S(2)}) copy-start(f32[64,512]{1,0:T(8,128)} %u.5) | copy-start | bytes 393220
  0.7 14.2 %copy-start.2 = (f32[64,512]{1,0:T(8,128)S(1)}, f32[64,512]{1,0:T(8,128)}, u32[]{:S(2)}) copy-start(f32[64,512]{1,0:T(8,128)} %v.5) | copy-start | bytes 393220
  0.7 14.2 %copy-start.3 = (f32[64,512]{1,0:T(8,128)S(1)}, f32[64,512]{1,0:T(8,128)}, u32[]{:S(2)}) copy-start(f32[64,512]{1,0:T(8,128)} %dx.5) | copy-start | bytes 393220
  0.7 14.2 %copy-start.4 = (f32[64,512]{1,0:T(8,128)S(1)}, f32[64,512]{1,0:T(8,128)}, u32[]{:S(2)}) copy-start(f32[64,512]{1,0:T(8,128)} %dy.5) | copy-start | bytes 393220
  1.7 7.8 %collective-permute-start = (f32[80,512]{1,0:T(8,128)S(1)}, f32[80,512]{1,0:T(8,128)S(1)}, u32[]{:S(2)}, u32[]{:S(2)}) collective-permute-start(f32[80,512]{1,0:T(8,128)S(1)} %get-tuple-element.12), channel_id=1, source_target_pairs={{0,32},{32,64},{64,96},{96,128},{128,160},{160,192},{192,224},{224... | collective-permute-start | bytes 491528 | tf_op jit(solution)/shard_map/ppermute | solution.py:243
  5.2 9.7 %collective-permute-start.1 = (f32[80,512]{1,0:T(8,128)S(1)}, f32[80,512]{1,0:T(8,128)S(1)}, u32[]{:S(2)}, u32[]{:S(2)}) collective-permute-start(f32[80,512]{1,0:T(8,128)S(1)} %get-tuple-element.13), channel_id=1, source_target_pairs={{32,0},{64,32},{96,64},{128,96},{160,128},{192,160},{224,192},{256... | collective-permute-start | bytes 491528 | tf_op jit(solution)/shard_map/ppermute | solution.py:244
  15.0 2.6 %collective-permute-start.2 = (f32[96,128]{1,0:T(8,128)S(1)}, f32[96,128]{1,0:T(8,128)S(1)}, u32[]{:S(2)}, u32[]{:S(2)}) collective-permute-start(f32[96,128]{1,0:T(8,128)S(1)} %get-tuple-element.14), channel_id=1, source_target_pairs={{0,1},{1,2},{2,3},{3,4},{4,5},{5,6},{6,7},{7,8},{8,9},{9,10},{10,1... | collective-permute-start | bytes 147464 | tf_op jit(solution)/shard_map/ppermute | solution.py:243
  16.3 5.3 %collective-permute-start.3 = (f32[96,128]{1,0:T(8,128)S(1)}, f32[96,128]{1,0:T(8,128)S(1)}, u32[]{:S(2)}, u32[]{:S(2)}) collective-permute-start(f32[96,128]{1,0:T(8,128)S(1)} %get-tuple-element.15), channel_id=1, source_target_pairs={{1,0},{2,1},{3,2},{4,3},{5,4},{6,5},{7,6},{8,7},{9,8},{10,9},{11,1... | collective-permute-start | bytes 147464 | tf_op jit(solution)/shard_map/ppermute | solution.py:244

commit v3 on v2

--- a/solution.py
+++ b/solution.py
@@ -9,7 +9,7 @@
 
 STEPS = 16
 GAUGE_DEV = 64
-QUAD = 4
+QUAD = 2
 LANES = 128
 DT = 0.45
 MIB = 1 << 20
@@ -63,7 +63,7 @@
 
 def steps_kernel(
     cells_in, place_x, place_y, ids_in, e, u, v, dx, dy, top, bot, from_left, from_right,
-    out_e, out_u, out_v, out_rec, he, hu, hv, sx, sy, cells, ids, staged, list_sems, out_sems,
+    out_e, out_u, out_v, out_rec, he, hu, hv, sx, sy, cells, ids, list_sems,
     *, steps, last_x, last_y,
 ):
     rows, cols = e.shape
@@ -110,22 +110,22 @@
     keep_rows = place_x[0] != last_x
     keep_cols = (lane8 >= LANES // 2) | (place_y[0] != last_y)
 
-    for s in range(steps):
-        low = (s // size) * size
-        now, new = s * pitch, (s + 1) * pitch
+    def one_step(low, s):
+        now = pl.multiple_of(s * pitch, 8)
+        new = pl.multiple_of(now + pitch, 8)
         flux_before = [None] * tiles
         for r in range(low, height - low, size):
-            eta = [he[j, now + r : now + r + size, :] for j in range(tiles)]
+            eta = [he[j, pl.ds(now + r, size), :] for j in range(tiles)]
             flux_y = []
             for j in range(tiles):
                 right = pltpu.roll(jnp.where(first_lane, eta[(j + 1) % tiles], eta[j]), LANES - 1, 1)
-                north = hv[j, now + r : now + r + size, :] - (right - eta[j])
-                hv[j, new + r : new + r + size, :] = north
+                north = hv[j, pl.ds(now + r, size), :] - (right - eta[j])
+                hv[j, pl.ds(new + r, size), :] = north
                 flux_y.append(sy[j, r : r + size, :] * north)
             for j in range(tiles):
-                down = he[j, now + r + 1 : now + r + 1 + size, :]
-                east = hu[j, now + r : now + r + size, :] - (down - eta[j])
-                hu[j, new + r : new + r + size, :] = east
+                down = he[j, pl.ds(now + r + 1, size), :]
+                east = hu[j, pl.ds(now + r, size), :] - (down - eta[j])
+                hu[j, pl.ds(new + r, size), :] = east
                 flux_x = sx[j, r : r + size, :] * east
                 above = flux_x if flux_before[j] is None else flux_before[j]
                 flux_up = pltpu.roll(jnp.where(final_row, above, flux_x), 1, 0)
@@ -136,22 +136,16 @@
                     after = jnp.where(keep_cols, after, 0.0)
                 if r >= rows + margin:
                     after = jnp.where(keep_rows, after, 0.0)
-                he[j, new + r : new + r + size, :] = after
+                he[j, pl.ds(new + r, size), :] = after
+
+    for low in range(0, steps, size):
+        lax.fori_loop(low, low + size, lambda s, _: one_step(low, s), None, unroll=1)
 
     last = steps * pitch + margin
-    outs = []
-    for j in range(own):
-        cut = pl.ds(LANES * j, LANES)
-        outs.append(pltpu.make_async_copy(hu.at[j, pl.ds(last, rows), :], out_u.at[:, cut], out_sems.at[j]))
-        outs.append(
-            pltpu.make_async_copy(hv.at[j, pl.ds(last, rows), :], out_v.at[:, cut], out_sems.at[own + j])
-        )
-    outs.append(pltpu.make_async_copy(staged, out_e, out_sems.at[2 * own]))
-    for copy in outs[:-1]:
-        copy.start()
-    for j in range(own):
-        staged[:, LANES * j : LANES * (j + 1)] = he[j, last : last + rows, :] * (1.0 / DT)
-    outs[-1].start()
+    for out, hist, factor in ((out_e, he, 1.0 / DT), (out_u, hu, None), (out_v, hv, None)):
+        for j in range(own):
+            value = hist[j, last : last + rows, :]
+            out[:, LANES * j : LANES * (j + 1)] = value if factor is None else value * factor
     for copy in lists:
         copy.wait()
 
@@ -174,12 +168,10 @@
         return tuple(out)
 
     zero = jnp.zeros((size, LANES), jnp.float32)
-    kept = lax.fori_loop(0, count, one_slot, (zero,) * (3 * groups), unroll=32)
+    kept = lax.fori_loop(0, count, one_slot, (zero,) * (3 * groups), unroll=128)
     for t, tile in enumerate(kept):
         out_rec[size * t : size * (t + 1), :] = tile * (1.0 / DT) if t < groups else tile
     out_rec[3 * steps : 3 * steps + 8, :] = jnp.broadcast_to(ids[...].astype(jnp.float32), (8, LANES))
-    for copy in outs:
-        copy.wait()
 
 
 def place_kernel(base, rec, out, *, series, members):
@@ -273,16 +265,14 @@
     depth = pltpu.VMEM((tiles, height, LANES), jnp.float32)
     eta, u, v, rec = pl.pallas_call(
         functools.partial(steps_kernel, steps=STEPS, last_x=n_gx - 1, last_y=n_gy - 1),
-        out_shape=(f32(rows, cols), f32(rows, cols), f32(rows, cols), f32(series + 8, LANES)),
+        out_shape=(pltpu.VMEM((rows, cols), jnp.float32),) * 3 + (f32(series + 8, LANES),),
         in_specs=[whole] + in_smem(2) + [whole] + in_vmem(9),
-        out_specs=(whole,) * 3 + tuple(in_vmem(1)),
+        out_specs=tuple(in_vmem(4)),
         scratch_shapes=[
             history, history, history, depth, depth,
             pltpu.SMEM(slot_cell.shape, jnp.int32),
             pltpu.VMEM(slot_gauge.shape, jnp.int32),
-            pltpu.VMEM((rows, cols), jnp.float32),
             pltpu.SemaphoreType.DMA((2,)),
-            pltpu.SemaphoreType.DMA((2 * tiles - 1,)),
         ],
         compiler_params=pltpu.CompilerParams(vmem_limit_bytes=24 * MIB),
         name="leapfrog",

time: 67.1 us -> 65.1 us (0.970)
  the two profiles are of different devices: /device:TPU:14 before, /device:TPU:46 now
where the time goes in v3:
time: 65.1 us; the launch traced here: 64.8 us
  starting transfers between devices  26.5 us (41%)
  waiting for transfers between devices  23.4 us (36%)
  Pallas kernels  8.58 us (13%)
  blocking collectives  3.55 us (5%)
  local copies, waits for them, and re-layouts  1.99 us (3%)
  between operations  0.77 us (1%)
    all_to_all x1, starting transfers between devices, shards(): lax.all_to_all(placed, 'gy', 0, 0, axis_index_groups=far, tiled=True)  15.1 us
    all_to_all x1, waiting for transfers between devices, shards(): lax.all_to_all(placed, 'gy', 0, 0, axis_index_groups=far, tiled=True)  14.5 us
    ppermute x2, waiting for transfers between devices, shifted(): lax.ppermute(head, axis, [(i + 1, i) for i in range(count - 1)])  6.94 us
    ppermute x2, starting transfers between devices, shifted(): lax.ppermute(head, axis, [(i + 1, i) for i in range(count - 1)])  6.09 us
    pallas_call x1, Pallas kernels, shards(): pl.pallas_call(functools.partial(steps_kernel, steps=STEPS, last_x=n_gx -...  5.54 us
    ppermute x2, starting transfers between devices, shifted(): lax.ppermute(tail, axis, [(i, i + 1) for i in range(count - 1)])  5.32 us
    all_gather x1, blocking collectives, shards(): gathered = lax.all_gather(rec, 'gy', axis_index_groups=near)  3.55 us
    unnamed x13, local copies, waits for them, and re-layouts  1.99 us
  transfers between devices with their start and end apart: 5, of which 4 were waited for; matrix products, arithmetic and copies ran while one was open for 3% of the time, Pallas kernels for 0%

profile of v3, /device:TPU:46, one launch (start us, length us, event | category | flops | bytes accessed | tf_op | source)
XLA Modules:
  0.0 64.8 jit_solution(13095825079526854278)
XLA Ops:
  0.6 0.0 copy-start
  0.6 0.0 copy-start.1
  0.7 0.0 copy-start.2
  0.7 0.0 copy-start.3
  0.7 0.0 copy-start.4
  0.7 1.1 %pack_rows.1 = (f32[80,512]{1,0:T(8,128)S(1)}, f32[80,512]{1,0:T(8,128)S(1)}) custom-call(f32[64,512]{1,0:T(8,128)} %e.5, f32[64,512]{1,0:T(8,128)} %u.5, f32[64,512]{1,0:T(8,128)} %v.5, f32[64,512]{1,0:T(8,128)} %dx.5, f32[64,512]{1,0:T(8,128)} %dy.5), custom_call_target="tpu_custom_call" | custom-call | tf_op jit(solution)/shard_map/pack_rows/pallas_call | solution.py:240
  1.7 3.4 %collective-permute-start = (f32[80,512]{1,0:T(8,128)S(1)}, f32[80,512]{1,0:T(8,128)S(1)}, u32[]{:S(2)}, u32[]{:S(2)}) collective-permute-start(f32[80,512]{1,0:T(8,128)S(1)} %get-tuple-element.12), channel_id=1, source_target_pairs={{0,32},{32,64},{64,96},{96,128},{128,160},{160,192},{192,224},{224... | collective-permute-start | bytes 491528 | tf_op jit(solution)/shard_map/ppermute | solution.py:235
  5.2 2.4 %collective-permute-start.1 = (f32[80,512]{1,0:T(8,128)S(1)}, f32[80,512]{1,0:T(8,128)S(1)}, u32[]{:S(2)}, u32[]{:S(2)}) collective-permute-start(f32[80,512]{1,0:T(8,128)S(1)} %get-tuple-element.13), channel_id=1, source_target_pairs={{32,0},{64,32},{96,64},{128,96},{160,128},{192,160},{224,192},{256... | collective-permute-start | bytes 491528 | tf_op jit(solution)/shard_map/ppermute | solution.py:236
  7.6 2.0 %collective-permute-done.top = f32[80,512]{1,0:T(8,128)S(1)} collective-permute-done((f32[80,512]{1,0:T(8,128)S(1)}, f32[80,512]{1,0:T(8,128)S(1)}, u32[]{:S(2)}, u32[]{:S(2)}) %collective-permute-start) | collective-permute-done | bytes 163872 | tf_op jit(solution)/shard_map/ppermute | solution.py:235
  9.6 5.2 %collective-permute-done.1.bot = f32[80,512]{1,0:T(8,128)S(1)} collective-permute-done((f32[80,512]{1,0:T(8,128)S(1)}, f32[80,512]{1,0:T(8,128)S(1)}, u32[]{:S(2)}, u32[]{:S(2)}) %collective-permute-start.1) | collective-permute-done | bytes 163872 | tf_op jit(solution)/shard_map/ppermute | solution.py:236
  14.8 0.0 copy-done
  14.8 0.0 copy-done.1
  14.8 0.0 copy-done.2
  14.8 0.0 copy-done.3
  14.8 0.0 copy-done.4
  14.8 0.2 pack_columns.1
  15.0 1.9 %collective-permute-start.2 = (f32[96,128]{1,0:T(8,128)S(1)}, f32[96,128]{1,0:T(8,128)S(1)}, u32[]{:S(2)}, u32[]{:S(2)}) collective-permute-start(f32[96,128]{1,0:T(8,128)S(1)} %get-tuple-element.14), channel_id=1, source_target_pairs={{0,1},{1,2},{2,3},{3,4},{4,5},{5,6},{6,7},{7,8},{8,9},{9,10},{10,1... | collective-permute-start | bytes 147464 | tf_op jit(solution)/shard_map/ppermute | solution.py:235
  17.0 3.6 %collective-permute-start.3 = (f32[96,128]{1,0:T(8,128)S(1)}, f32[96,128]{1,0:T(8,128)S(1)}, u32[]{:S(2)}, u32[]{:S(2)}) collective-permute-start(f32[96,128]{1,0:T(8,128)S(1)} %get-tuple-element.15), channel_id=1, source_target_pairs={{1,0},{2,1},{3,2},{4,3},{5,4},{6,5},{7,6},{8,7},{9,8},{10,9},{11,1... | collective-permute-start | bytes 147464 | tf_op jit(solution)/shard_map/ppermute | solution.py:236
  20.6 0.0 collective-permute-done.2.from_left
  20.6 1.7 %collective-permute-done.3.from_right = f32[96,128]{1,0:T(8,128)S(1)} collective-permute-done((f32[96,128]{1,0:T(8,128)S(1)}, f32[96,128]{1,0:T(8,128)S(1)}, u32[]{:S(2)}, u32[]{:S(2)}) %collective-permute-start.3) | collective-permute-done | bytes 49184 | tf_op jit(solution)/shard_map/ppermute | solution.py:236
  22.3 5.5 %leapfrog.1 = (f32[64,512]{1,0:T(8,128)S(1)}, f32[64,512]{1,0:T(8,128)S(1)}, f32[64,512]{1,0:T(8,128)S(1)}, f32[56,128]{1,0:T(8,128)S(1)}) custom-call(s32[1,128]{1,0:T(1,128)} %cells_in.1, s32[1]{0:T(128)} %bitcast.place_x, s32[1]{0:T(128)} %bitcast.1.place_y, s32[1,128]{1,0:T(1,128)} %ids_in.1, f32[64,512]{1,0:T(8,128)S(1)} %copy-done, ...), custom_call_target="tpu_custom_call" | custom-call | tf_op jit(solution)/shard_map/leapfrog/pallas_call | solution.py:266
  27.9 3.5 %all-gather = f32[112,128]{1,0:T(8,128)S(1)} all-gather(f32[56,128]{1,0:T(8,128)S(1)} %get-tuple-element.19), channel_id=2, replica_groups={{0,1},{2,3},{4,5},{6,7},{8,9},{10,11},{12,13},{14,15},{16,17},{18,19},{..., dimensions={0}, use_global_device_ids=true | all-gather | bytes 86016 | tf_op jit(solution)/shard_map/all_gather | solution.py:290
  31.4 1.1 %place.1 = f32[16,24,128]{2,1,0:T(8,128)} custom-call(s32[1]{0:T(128)} %bitcast.2.base, f32[2,56,128]{2,1,0:T(8,128)S(1)} %bitcast.5), custom_call_target="tpu_custom_call" | custom-call | tf_op jit(solution)/shard_map/place/pallas_call | solution.py:293
  32.5 15.1 %all-to-all-start = ((f32[16,24,128]{2,1,0:T(8,128)}), f32[16,24,128]{2,1,0:T(8,128)S(1)}, u32[]{:S(2)}, u32[]{:S(2)}) async-start(f32[16,24,128]{2,1,0:T(8,128)} %place.1), calls=%async_computation | async-start | bytes 393216 | tf_op jit(solution)/shard_map/all_to_all | solution.py:301
  47.6 0.7 %copy.11 = f32[64,512]{1,0:T(8,128)} copy(f32[64,512]{1,0:T(8,128)S(1)} %get-tuple-element.20) | data formatting | bytes 262144
  48.3 0.7 %copy.12 = f32[64,512]{1,0:T(8,128)} copy(f32[64,512]{1,0:T(8,128)S(1)} %get-tuple-element.21) | data formatting | bytes 262144
  48.9 0.7 %copy.13 = f32[64,512]{1,0:T(8,128)} copy(f32[64,512]{1,0:T(8,128)S(1)} %get-tuple-element.22) | data formatting | bytes 262144
  49.6 14.5 %all-to-all-done.parts = f32[16,24,128]{2,1,0:T(8,128)S(1)} async-done(((f32[16,24,128]{2,1,0:T(8,128)}), f32[16,24,128]{2,1,0:T(8,128)S(1)}, u32[]{:S(2)}, u32[]{:S(2)}) %all-to-all-start) | async-done | bytes 196640 | tf_op jit(solution)/shard_map/all_to_all | solution.py:301
  64.1 0.7 %finish.1 = f32[48,64]{1,0:T(8,128)} custom-call(f32[16,24,128]{2,1,0:T(8,128)S(1)} %all-to-all-done.parts), custom_call_target="tpu_custom_call" | custom-call | tf_op jit(solution)/shard_map/finish/pallas_call | solution.py:302
Async XLA Ops:
  0.6 14.2 %copy-start = (f32[64,512]{1,0:T(8,128)S(1)}, f32[64,512]{1,0:T(8,128)}, u32[]{:S(2)}) copy-start(f32[64,512]{1,0:T(8,128)} %e.5) | copy-start | bytes 393220
  0.6 14.2 %copy-start.1 = (f32[64,512]{1,0:T(8,128)S(1)}, f32[64,512]{1,0:T(8,128)}, u32[]{:S(2)}) copy-start(f32[64,512]{1,0:T(8,128)} %u.5) | copy-start | bytes 393220
  0.7 14.2 %copy-start.2 = (f32[64,512]{1,0:T(8,128)S(1)}, f32[64,512]{1,0:T(8,128)}, u32[]{:S(2)}) copy-start(f32[64,512]{1,0:T(8,128)} %v.5) | copy-start | bytes 393220
  0.7 14.2 %copy-start.3 = (f32[64,512]{1,0:T(8,128)S(1)}, f32[64,512]{1,0:T(8,128)}, u32[]{:S(2)}) copy-start(f32[64,512]{1,0:T(8,128)} %dx.5) | copy-start | bytes 393220
  0.7 14.2 %copy-start.4 = (f32[64,512]{1,0:T(8,128)S(1)}, f32[64,512]{1,0:T(8,128)}, u32[]{:S(2)}) copy-start(f32[64,512]{1,0:T(8,128)} %dy.5) | copy-start | bytes 393220
  1.7 7.8 %collective-permute-start = (f32[80,512]{1,0:T(8,128)S(1)}, f32[80,512]{1,0:T(8,128)S(1)}, u32[]{:S(2)}, u32[]{:S(2)}) collective-permute-start(f32[80,512]{1,0:T(8,128)S(1)} %get-tuple-element.12), channel_id=1, source_target_pairs={{0,32},{32,64},{64,96},{96,128},{128,160},{160,192},{192,224},{224... | collective-permute-start | bytes 491528 | tf_op jit(solution)/shard_map/ppermute | solution.py:235
  5.2 9.7 %collective-permute-start.1 = (f32[80,512]{1,0:T(8,128)S(1)}, f32[80,512]{1,0:T(8,128)S(1)}, u32[]{:S(2)}, u32[]{:S(2)}) collective-permute-start(f32[80,512]{1,0:T(8,128)S(1)} %get-tuple-element.13), channel_id=1, source_target_pairs={{32,0},{64,32},{96,64},{128,96},{160,128},{192,160},{224,192},{256... | collective-permute-start | bytes 491528 | tf_op jit(solution)/shard_map/ppermute | solution.py:236
  15.0 5.6 %collective-permute-start.2 = (f32[96,128]{1,0:T(8,128)S(1)}, f32[96,128]{1,0:T(8,128)S(1)}, u32[]{:S(2)}, u32[]{:S(2)}) collective-permute-start(f32[96,128]{1,0:T(8,128)S(1)} %get-tuple-element.14), channel_id=1, source_target_pairs={{0,1},{1,2},{2,3},{3,4},{4,5},{5,6},{6,7},{7,8},{8,9},{9,10},{10,1... | collective-permute-start | bytes 147464 | tf_op jit(solution)/shard_map/ppermute | solution.py:235
  17.0 5.4 %collective-permute-start.3 = (f32[96,128]{1,0:T(8,128)S(1)}, f32[96,128]{1,0:T(8,128)S(1)}, u32[]{:S(2)}, u32[]{:S(2)}) collective-permute-start(f32[96,128]{1,0:T(8,128)S(1)} %get-tuple-element.15), channel_id=1, source_target_pairs={{1,0},{2,1},{3,2},{4,3},{5,4},{6,5},{7,6},{8,7},{9,8},{10,9},{11,1... | collective-permute-start | bytes 147464 | tf_op jit(solution)/shard_map/ppermute | solution.py:236
  32.5 31.5 %all-to-all-start = ((f32[16,24,128]{2,1,0:T(8,128)}), f32[16,24,128]{2,1,0:T(8,128)S(1)}, u32[]{:S(2)}, u32[]{:S(2)}) async-start(f32[16,24,128]{2,1,0:T(8,128)} %place.1), calls=%async_computation | async-start | bytes 393216 | tf_op jit(solution)/shard_map/all_to_all | solution.py:301

commit v4 on v2

--- a/solution.py
+++ b/solution.py
@@ -9,7 +9,6 @@
 
 STEPS = 16
 GAUGE_DEV = 64
-QUAD = 4
 LANES = 128
 DT = 0.45
 MIB = 1 << 20
@@ -19,7 +18,8 @@
     return lax.broadcasted_iota(jnp.int32, shape, 1)
 
 
-def pack_columns_kernel(e, u, v, dx, dy, top, bot, head, tail, *, margin):
+def pack_columns_kernel(place_y, e, u, v, dx, dy, top, bot, near, far, *, margin):
+    even = place_y[0] % 2 == 0
     rows, cols = e.shape
     lane = lane_ids((margin, LANES))
     last = cols - LANES
@@ -42,8 +42,8 @@
             final = pltpu.roll(final, (margin * f + margin) % LANES, 1)
             out_head = jnp.where(mine, first, out_head)
             out_tail = jnp.where(mine, final, out_tail)
-        head[r : r + margin, :] = out_head
-        tail[r : r + margin, :] = out_tail
+        near[r : r + margin, :] = jnp.where(even, out_tail, out_head)
+        far[r : r + margin, :] = jnp.where(even, out_head, out_tail)
 
 
 def pack_rows_kernel(e, u, v, dx, dy, head, tail, sems, *, margin):
@@ -62,7 +62,7 @@
 
 
 def steps_kernel(
-    cells_in, place_x, place_y, ids_in, e, u, v, dx, dy, top, bot, from_left, from_right,
+    cells_in, place_x, place_y, ids_in, e, u, v, dx, dy, top, bot, from_near, from_far,
     out_e, out_u, out_v, out_rec, he, hu, hv, sx, sy, cells, ids, staged, list_sems, out_sems,
     *, steps, last_x, last_y,
 ):
@@ -74,6 +74,7 @@
     pitch = height + 8
     chunk = 16
     lane = lane_ids((chunk, LANES))
+    even = place_y[0] % 2 == 0
     lists = [
         pltpu.make_async_copy(cells_in, cells, list_sems.at[0]),
         pltpu.make_async_copy(ids_in, ids, list_sems.at[1]),
@@ -93,8 +94,9 @@
             dst[j, margin : margin + rows, :] = scaled(ref[:, cut])
             dst[j, margin + rows : height, :] = scaled(bot[f * margin : (f + 1) * margin, cut])
         for r in range(0, height, chunk):
-            right = from_right[r : r + chunk, :]
-            left = from_left[r : r + chunk, :]
+            crossed = from_far[r : r + chunk, :]
+            right = jnp.where(even, from_near[1, r : r + chunk, :], crossed)
+            left = jnp.where(even, crossed, from_near[0, r : r + chunk, :])
             if f:
                 right = pltpu.roll(right, LANES - margin * f, 1)
             left = pltpu.roll(left, (LANES - margin - margin * f) % LANES, 1)
@@ -110,22 +112,22 @@
     keep_rows = place_x[0] != last_x
     keep_cols = (lane8 >= LANES // 2) | (place_y[0] != last_y)
 
-    for s in range(steps):
-        low = (s // size) * size
-        now, new = s * pitch, (s + 1) * pitch
+    def one_step(low, s):
+        now = pl.multiple_of(s * pitch, 8)
+        new = pl.multiple_of(now + pitch, 8)
         flux_before = [None] * tiles
         for r in range(low, height - low, size):
-            eta = [he[j, now + r : now + r + size, :] for j in range(tiles)]
+            eta = [he[j, pl.ds(now + r, size), :] for j in range(tiles)]
             flux_y = []
             for j in range(tiles):
                 right = pltpu.roll(jnp.where(first_lane, eta[(j + 1) % tiles], eta[j]), LANES - 1, 1)
-                north = hv[j, now + r : now + r + size, :] - (right - eta[j])
-                hv[j, new + r : new + r + size, :] = north
+                north = hv[j, pl.ds(now + r, size), :] - (right - eta[j])
+                hv[j, pl.ds(new + r, size), :] = north
                 flux_y.append(sy[j, r : r + size, :] * north)
             for j in range(tiles):
-                down = he[j, now + r + 1 : now + r + 1 + size, :]
-                east = hu[j, now + r : now + r + size, :] - (down - eta[j])
-                hu[j, new + r : new + r + size, :] = east
+                down = he[j, pl.ds(now + r + 1, size), :]
+                east = hu[j, pl.ds(now + r, size), :] - (down - eta[j])
+                hu[j, pl.ds(new + r, size), :] = east
                 flux_x = sx[j, r : r + size, :] * east
                 above = flux_x if flux_before[j] is None else flux_before[j]
                 flux_up = pltpu.roll(jnp.where(final_row, above, flux_x), 1, 0)
@@ -136,7 +138,10 @@
                     after = jnp.where(keep_cols, after, 0.0)
                 if r >= rows + margin:
                     after = jnp.where(keep_rows, after, 0.0)
-                he[j, new + r : new + r + size, :] = after
+                he[j, pl.ds(new + r, size), :] = after
+
+    for low in range(0, steps, size):
+        lax.fori_loop(low, low + size, lambda s, _: one_step(low, s), None, unroll=1)
 
     last = steps * pitch + margin
     outs = []
@@ -174,7 +179,7 @@
         return tuple(out)
 
     zero = jnp.zeros((size, LANES), jnp.float32)
-    kept = lax.fori_loop(0, count, one_slot, (zero,) * (3 * groups), unroll=32)
+    kept = lax.fori_loop(0, count, one_slot, (zero,) * (3 * groups), unroll=128)
     for t, tile in enumerate(kept):
         out_rec[size * t : size * (t + 1), :] = tile * (1.0 / DT) if t < groups else tile
     out_rec[3 * steps : 3 * steps + 8, :] = jnp.broadcast_to(ids[...].astype(jnp.float32), (8, LANES))
@@ -239,11 +244,6 @@
     a, b = lax.axis_index("gx"), lax.axis_index("gy")
     fields = (surface, east, north, east_depth, north_depth)
 
-    def shifted(tail, head, axis, count):
-        from_before = lax.ppermute(tail, axis, [(i, i + 1) for i in range(count - 1)])
-        from_after = lax.ppermute(head, axis, [(i + 1, i) for i in range(count - 1)])
-        return from_before, from_after
-
     whole = pl.BlockSpec(memory_space=pltpu.HBM)
     head_rows, tail_rows = pl.pallas_call(
         functools.partial(pack_rows_kernel, margin=margin),
@@ -254,18 +254,24 @@
         compiler_params=pltpu.CompilerParams(vmem_limit_bytes=4 * MIB),
         name="pack_rows",
     )(*(pltpu.with_memory_space_constraint(f, pltpu.HBM) for f in fields))
-    top, bot = shifted(tail_rows, head_rows, "gx", n_gx)
+    top = lax.ppermute(tail_rows, "gx", [(i, i + 1) for i in range(n_gx - 1)])
+    bot = lax.ppermute(head_rows, "gx", [(i + 1, i) for i in range(n_gx - 1)])
 
     height = rows + 2 * margin
-    head, tail = pl.pallas_call(
+    place_x = a.astype(jnp.int32).reshape(1)
+    place_y = b.astype(jnp.int32).reshape(1)
+    near, far = pl.pallas_call(
         functools.partial(pack_columns_kernel, margin=margin),
         out_shape=(f32(height, LANES), f32(height, LANES)),
-        in_specs=in_vmem(7),
+        in_specs=in_smem(1) + in_vmem(7),
         out_specs=tuple(in_vmem(2)),
         compiler_params=pltpu.CompilerParams(vmem_limit_bytes=4 * MIB),
         name="pack_columns",
-    )(*fields, top, bot)
-    from_left, from_right = shifted(tail, head, "gy", n_gy)
+    )(place_y, *fields, top, bot)
+    bonds = [(i, i + 1) for i in range(1, n_gy - 1, 2)]
+    pairs = [[2 * i, 2 * i + 1] for i in range(n_gy // 2)]
+    from_far = lax.ppermute(far, "gy", bonds + [(j, i) for i, j in bonds])
+    from_near = lax.all_gather(near, "gy", axis_index_groups=pairs)
 
     tiles = cols // LANES + 1
     pitch = height + 8
@@ -273,7 +279,7 @@
     depth = pltpu.VMEM((tiles, height, LANES), jnp.float32)
     eta, u, v, rec = pl.pallas_call(
         functools.partial(steps_kernel, steps=STEPS, last_x=n_gx - 1, last_y=n_gy - 1),
-        out_shape=(f32(rows, cols), f32(rows, cols), f32(rows, cols), f32(series + 8, LANES)),
+        out_shape=(f32(rows, cols),) * 3 + (f32(series + 8, LANES),),
         in_specs=[whole] + in_smem(2) + [whole] + in_vmem(9),
         out_specs=(whole,) * 3 + tuple(in_vmem(1)),
         scratch_shapes=[
@@ -288,17 +294,16 @@
         name="leapfrog",
     )(
         pltpu.with_memory_space_constraint(slot_cell, pltpu.HBM),
-        a.astype(jnp.int32).reshape(1),
-        b.astype(jnp.int32).reshape(1),
+        place_x,
+        place_y,
         pltpu.with_memory_space_constraint(slot_gauge, pltpu.HBM),
-        *fields, top, bot, from_left, from_right,
+        *fields, top, bot, from_near, from_far,
     )
 
-    near = [[QUAD * i + j for j in range(QUAD)] for i in range(n_gy // QUAD)]
-    members = n_gy // QUAD
-    far = [[i + QUAD * j for j in range(members)] for i in range(QUAD)]
-    gathered = lax.all_gather(rec, "gy", axis_index_groups=near)
-    base = (a * (n_gy * GAUGE_DEV) + (b % QUAD) * GAUGE_DEV).astype(jnp.int32).reshape(1)
+    members = n_gy // 2
+    chips = [[i + 2 * j for j in range(members)] for i in range(2)]
+    gathered = lax.all_gather(rec, "gy", axis_index_groups=pairs)
+    base = (a * (n_gy * GAUGE_DEV) + (b % 2) * GAUGE_DEV).astype(jnp.int32).reshape(1)
     half = series // 2
     placed = pl.pallas_call(
         functools.partial(place_kernel, series=series, members=members),
@@ -308,7 +313,7 @@
         compiler_params=pltpu.CompilerParams(vmem_limit_bytes=8 * MIB),
         name="place",
     )(base, gathered)
-    arrived = lax.all_to_all(placed, "gy", 0, 0, axis_index_groups=far, tiled=True)
+    arrived = lax.all_to_all(placed, "gy", 0, 0, axis_index_groups=chips, tiled=True)
     out = pl.pallas_call(
         functools.partial(finish_kernel, series=series),
         out_shape=f32(series, GAUGE_DEV),

time: 67.1 us -> 61.8 us (0.921)
  the two profiles are of different devices: /device:TPU:14 before, /device:TPU:38 now
where the time goes in v4:
time: 61.8 us; the launch traced here: 61.5 us
  blocking collectives  37.8 us (61%)
  Pallas kernels  7.98 us (13%)
  starting transfers between devices  7.76 us (13%)
  waiting for transfers between devices  7.21 us (12%)
  between operations  0.77 us (1%)
    all_to_all x1, blocking collectives, shards(): lax.all_to_all(placed, 'gy', 0, 0, axis_index_groups=chips, tiled=True)  32.4 us
    pallas_call x1, Pallas kernels, shards(): pl.pallas_call(functools.partial(steps_kernel, steps=STEPS, last_x=n_gx -...  5.63 us
    ppermute x1, waiting for transfers between devices, shards(): bot = lax.ppermute(head_rows, 'gx', [(i + 1, i) for i in range(n_gx - 1)])  5.24 us
    all_gather x1, blocking collectives, shards(): from_near = lax.all_gather(near, 'gy', axis_index_groups=pairs)  3.54 us
    ppermute x1, starting transfers between devices, shards(): top = lax.ppermute(tail_rows, 'gx', [(i, i + 1) for i in range(n_gx - 1)])  3.4 us
    ppermute x1, starting transfers between devices, shards(): bot = lax.ppermute(head_rows, 'gx', [(i + 1, i) for i in range(n_gx - 1)])  2.44 us
    ppermute x1, waiting for transfers between devices, shards(): top = lax.ppermute(tail_rows, 'gx', [(i, i + 1) for i in range(n_gx - 1)])  1.97 us
    ppermute x1, starting transfers between devices, shards(): from_far = lax.ppermute(far, 'gy', bonds + [(j, i) for i, j in bonds])  1.92 us
  transfers between devices with their start and end apart: 3, of which 2 were waited for; matrix products, arithmetic and copies ran while one was open for 0% of the time, Pallas kernels for 0%

profile of v4, /device:TPU:38, one launch (start us, length us, event | category | flops | bytes accessed | tf_op | source)
XLA Modules:
  0.0 61.5 jit_solution(5590328304432305891)
XLA Ops:
  0.6 0.0 copy-start
  0.6 0.0 copy-start.1
  0.7 0.0 copy-start.2
  0.7 0.0 copy-start.3
  0.7 0.0 copy-start.4
  0.7 1.1 %pack_rows.1 = (f32[80,512]{1,0:T(8,128)S(1)}, f32[80,512]{1,0:T(8,128)S(1)}) custom-call(f32[64,512]{1,0:T(8,128)} %e.5, f32[64,512]{1,0:T(8,128)} %u.5, f32[64,512]{1,0:T(8,128)} %v.5, f32[64,512]{1,0:T(8,128)} %dx.5, f32[64,512]{1,0:T(8,128)} %dy.5), custom_call_target="tpu_custom_call" | custom-call | tf_op jit(solution)/shard_map/pack_rows/pallas_call | solution.py:248
  1.7 3.4 %collective-permute-start = (f32[80,512]{1,0:T(8,128)S(1)}, f32[80,512]{1,0:T(8,128)S(1)}, u32[]{:S(2)}, u32[]{:S(2)}) collective-permute-start(f32[80,512]{1,0:T(8,128)S(1)} %get-tuple-element.12), channel_id=1, source_target_pairs={{0,32},{32,64},{64,96},{96,128},{128,160},{160,192},{192,224},{224... | collective-permute-start | bytes 491528 | tf_op jit(solution)/shard_map/ppermute | solution.py:257
  5.2 2.4 %collective-permute-start.1 = (f32[80,512]{1,0:T(8,128)S(1)}, f32[80,512]{1,0:T(8,128)S(1)}, u32[]{:S(2)}, u32[]{:S(2)}) collective-permute-start(f32[80,512]{1,0:T(8,128)S(1)} %get-tuple-element.13), channel_id=1, source_target_pairs={{32,0},{64,32},{96,64},{128,96},{160,128},{192,160},{224,192},{256... | collective-permute-start | bytes 491528 | tf_op jit(solution)/shard_map/ppermute | solution.py:258
  7.6 2.0 %collective-permute-done.top = f32[80,512]{1,0:T(8,128)S(1)} collective-permute-done((f32[80,512]{1,0:T(8,128)S(1)}, f32[80,512]{1,0:T(8,128)S(1)}, u32[]{:S(2)}, u32[]{:S(2)}) %collective-permute-start) | collective-permute-done | bytes 163872 | tf_op jit(solution)/shard_map/ppermute | solution.py:257
  9.6 5.2 %collective-permute-done.1.bot = f32[80,512]{1,0:T(8,128)S(1)} collective-permute-done((f32[80,512]{1,0:T(8,128)S(1)}, f32[80,512]{1,0:T(8,128)S(1)}, u32[]{:S(2)}, u32[]{:S(2)}) %collective-permute-start.1) | collective-permute-done | bytes 163872 | tf_op jit(solution)/shard_map/ppermute | solution.py:258
  14.8 0.0 copy-done
  14.8 0.0 copy-done.1
  14.8 0.0 copy-done.2
  14.8 0.0 copy-done.3
  14.8 0.0 copy-done.4
  14.8 0.2 pack_columns.1
  15.0 1.9 %collective-permute-start.2 = (f32[96,128]{1,0:T(8,128)S(1)}, f32[96,128]{1,0:T(8,128)S(1)}, u32[]{:S(2)}, u32[]{:S(2)}) collective-permute-start(f32[96,128]{1,0:T(8,128)S(1)} %get-tuple-element.15), channel_id=1, source_target_pairs={{1,2},{3,4},{5,6},{7,8},{9,10},{11,12},{13,14},{15,16},{17,18},{19... | collective-permute-start | bytes 147464 | tf_op jit(solution)/shard_map/ppermute | solution.py:273
  17.0 3.5 %all-gather = f32[192,128]{1,0:T(8,128)S(1)} all-gather(f32[96,128]{1,0:T(8,128)S(1)} %get-tuple-element.14), channel_id=2, replica_groups={{0,1},{2,3},{4,5},{6,7},{8,9},{10,11},{12,13},{14,15},{16,17},{18,19},{..., dimensions={0}, use_global_device_ids=true | all-gather | bytes 147456 | tf_op jit(solution)/shard_map/all_gather | solution.py:274
  20.5 0.0 collective-permute-done.2.from_far
  20.5 5.6 %leapfrog.1 = (f32[64,512]{1,0:T(8,128)}, f32[64,512]{1,0:T(8,128)}, f32[64,512]{1,0:T(8,128)}, f32[56,128]{1,0:T(8,128)S(1)}) custom-call(s32[1,128]{1,0:T(1,128)} %cells_in.1, s32[1]{0:T(128)} %bitcast.place_x, s32[1]{0:T(128)} %bitcast.1.place_y, s32[1,128]{1,0:T(1,128)} %ids_in.1, f32[64,512]{1,0:T(8,128)S(1)} %copy-done, f32[64,512]{1,0:T(8,128)S(1)} %copy-done.1, ...), custom_call_target="tpu_custom_call" | custom-call | tf_op jit(solution)/shard_map/leapfrog/pallas_call | solution.py:280
  26.2 1.9 %all-gather.1 = f32[112,128]{1,0:T(8,128)S(1)} all-gather(f32[56,128]{1,0:T(8,128)S(1)} %get-tuple-element.19), channel_id=3, replica_groups={{0,1},{2,3},{4,5},{6,7},{8,9},{10,11},{12,13},{14,15},{16,17},{18,19},{..., dimensions={0}, use_global_device_ids=true | all-gather | bytes 86016 | tf_op jit(solution)/shard_map/all_gather | solution.py:305
  28.0 0.4 place.1
  28.4 32.4 %all_to_all.5.parts = f32[16,24,128]{2,1,0:T(8,128)S(1)} all-to-all(f32[16,24,128]{2,1,0:T(8,128)S(1)} %place.1), channel_id=1, replica_groups={{0,2,4,6,8,10,12,14,16,18,20,22,24,26,28,30},{1,3,5,7,9,11,13,15,17,19,..., dimensions={0} | all-to-all | bytes 393216 | tf_op jit(solution)/shard_map/all_to_all | solution.py:316
  60.8 0.7 %finish.1 = f32[48,64]{1,0:T(8,128)} custom-call(f32[16,24,128]{2,1,0:T(8,128)S(1)} %all_to_all.5.parts), custom_call_target="tpu_custom_call" | custom-call | tf_op jit(solution)/shard_map/finish/pallas_call | solution.py:317
Async XLA Ops:
  0.6 14.2 %copy-start = (f32[64,512]{1,0:T(8,128)S(1)}, f32[64,512]{1,0:T(8,128)}, u32[]{:S(2)}) copy-start(f32[64,512]{1,0:T(8,128)} %e.5) | copy-start | bytes 393220
  0.6 14.2 %copy-start.1 = (f32[64,512]{1,0:T(8,128)S(1)}, f32[64,512]{1,0:T(8,128)}, u32[]{:S(2)}) copy-start(f32[64,512]{1,0:T(8,128)} %u.5) | copy-start | bytes 393220
  0.7 14.2 %copy-start.2 = (f32[64,512]{1,0:T(8,128)S(1)}, f32[64,512]{1,0:T(8,128)}, u32[]{:S(2)}) copy-start(f32[64,512]{1,0:T(8,128)} %v.5) | copy-start | bytes 393220
  0.7 14.2 %copy-start.3 = (f32[64,512]{1,0:T(8,128)S(1)}, f32[64,512]{1,0:T(8,128)}, u32[]{:S(2)}) copy-start(f32[64,512]{1,0:T(8,128)} %dx.5) | copy-start | bytes 393220
  0.7 14.2 %copy-start.4 = (f32[64,512]{1,0:T(8,128)S(1)}, f32[64,512]{1,0:T(8,128)}, u32[]{:S(2)}) copy-start(f32[64,512]{1,0:T(8,128)} %dy.5) | copy-start | bytes 393220
  1.7 7.8 %collective-permute-start = (f32[80,512]{1,0:T(8,128)S(1)}, f32[80,512]{1,0:T(8,128)S(1)}, u32[]{:S(2)}, u32[]{:S(2)}) collective-permute-start(f32[80,512]{1,0:T(8,128)S(1)} %get-tuple-element.12), channel_id=1, source_target_pairs={{0,32},{32,64},{64,96},{96,128},{128,160},{160,192},{192,224},{224... | collective-permute-start | bytes 491528 | tf_op jit(solution)/shard_map/ppermute | solution.py:257
  5.2 9.7 %collective-permute-start.1 = (f32[80,512]{1,0:T(8,128)S(1)}, f32[80,512]{1,0:T(8,128)S(1)}, u32[]{:S(2)}, u32[]{:S(2)}) collective-permute-start(f32[80,512]{1,0:T(8,128)S(1)} %get-tuple-element.13), channel_id=1, source_target_pairs={{32,0},{64,32},{96,64},{128,96},{160,128},{192,160},{224,192},{256... | collective-permute-start | bytes 491528 | tf_op jit(solution)/shard_map/ppermute | solution.py:258
  15.0 5.5 %collective-permute-start.2 = (f32[96,128]{1,0:T(8,128)S(1)}, f32[96,128]{1,0:T(8,128)S(1)}, u32[]{:S(2)}, u32[]{:S(2)}) collective-permute-start(f32[96,128]{1,0:T(8,128)S(1)} %get-tuple-element.15), channel_id=1, source_target_pairs={{1,2},{3,4},{5,6},{7,8},{9,10},{11,12},{13,14},{15,16},{17,18},{19... | collective-permute-start | bytes 147464 | tf_op jit(solution)/shard_map/ppermute | solution.py:273
